TPU v7x, 512 devices: a whole 4x4x16 slice. The times are simulated.
512 devices in a mesh: harm: 4 (over z_hi, core), tx: 16 (over y, x), ty: 8 (over z_lo).
Axes of the slice: x: 4, y: 4, z: 16 (z_hi: 2, z_lo: 8; z = z_hi * 8 + z_lo), core: 2. Of those that a mesh axis runs over, the one named last changes fastest.
Arguments:
- wave_spectrum: float32 [2, 512, 64, 1024], P(None, 'harm', 'tx', 'ty'), may hold values from -6 to 6
- lens_window: int32 [64, 1024], P('tx', 'ty'), may hold values 0 or 1
- medium_label: int32 [64, 1024], P('tx', 'ty'), may hold values from 0 to 7
- thermal_excess_prior: float32 [64, 1024], P('tx', 'ty'), may hold values from -6 to 6
- attenuation_by_kind: float32 [8], replicated, may hold values from 0.2 to 2
- blood_drain_by_kind: float32 [8], replicated, may hold values from 0.02 to 0.2
- diffusivity_by_kind: float32 [8], replicated, may hold values from 0.04 to 0.22
Outputs:
- field_out: float32 [2, 512, 64, 1024], P(None, 'harm', 'tx', 'ty')
- thermal_excess_later: float32 [64, 1024], P('tx', 'ty')
All inputs are finite; a program needn't handle non-finite values. No bound on the sum of `lens_window` on one device may be relied on, other than what follows from the above.
Results may differ from a plain program's by a relative error of at most 0.000071.
Values sent between devices are 32-bit elements; how exact they have to be, the bound alone decides.
A program may use at most 64 MiB of HBM per device.

v0:
```python
import math

import jax
import jax.numpy as jnp
from jax import lax
from jax.sharding import Mesh
from jax.sharding import PartitionSpec as P

CYCLE_READINGS = 2048
HARM = ("harm_0", "harm_1")


diffraction_gain = 0.3
nonlinear_gain = 0.3


def extended(block, sides, width):
    for axis, dim in sides:
        count = lax.axis_size(axis)
        forward = [(i, i + 1) for i in range(count - 1)]
        backward = [(target, source) for source, target in forward]
        low = lax.ppermute(
            lax.slice_in_dim(block, block.shape[dim] - width, None, axis=dim), axis, forward
        )
        high = lax.ppermute(lax.slice_in_dim(block, 0, width, axis=dim), axis, backward)
        block = jnp.concatenate([low, block, high], axis=dim)
    return block


def in_order(pieces, dim):
    shape = list(pieces.shape[1:])
    shape[dim] *= pieces.shape[0]
    return jnp.moveaxis(pieces, 0, dim).reshape(shape)


def all_blocks(array, axes, sequence):
    pieces = array
    for k in sequence:
        pieces = lax.all_gather(pieces, axes[k])
    done = sequence[::-1]
    back = [done.index(k) for k in range(len(axes))]
    pieces = pieces.transpose(*back, *range(len(axes), pieces.ndim))
    return pieces.reshape(-1, *array.shape)


def gather_axes(array, axes, sequence, dim):
    return in_order(all_blocks(array, axes, sequence), dim)


def laplace(padded):
    center = padded[..., 1:-1, 1:-1]
    return (
        padded[..., 2:, 1:-1]
        + padded[..., :-2, 1:-1]
        + padded[..., 1:-1, 2:]
        + padded[..., 1:-1, :-2]
        - 4.0 * center
    )


def build_table(overall):
    moment_grid = jnp.arange(CYCLE_READINGS, dtype=jnp.int32)
    overtone_series = jnp.arange(1, overall + 1, dtype=jnp.int32)
    cycle_argument = moment_grid[:, None] * overtone_series[None, :] % CYCLE_READINGS
    angle = 2.0 * math.pi / CYCLE_READINGS * cycle_argument.astype(jnp.float32)
    return jnp.concatenate([jnp.cos(angle), -jnp.sin(angle)], axis=1)


def inside_grid(height, breadth, margin):
    row_index = (
        lax.axis_index("tx") * height - margin + jnp.arange(height + 2 * margin, dtype=jnp.int32)
    )
    col_index = (
        lax.axis_index("ty") * breadth - margin + jnp.arange(breadth + 2 * margin, dtype=jnp.int32)
    )
    row_valid = (row_index >= 0) & (row_index < height * lax.axis_size("tx"))
    col_valid = (col_index >= 0) & (col_index < breadth * lax.axis_size("ty"))
    return (row_valid[:, None] & col_valid[None, :]).astype(jnp.float32)


def body(
    wave_spectrum,
    lens_window,
    medium_label,
    thermal_excess_prior,
    attenuation_by_kind,
    blood_drain_by_kind,
    diffusivity_by_kind,
):
    own_count = wave_spectrum.shape[1]
    height = wave_spectrum.shape[2]
    breadth = wave_spectrum.shape[3]
    overall = own_count * lax.axis_size(HARM)
    orders = (
        lax.axis_index(HARM) * own_count + jnp.arange(1, own_count + 1, dtype=jnp.int32)
    ).astype(jnp.float32)
    weight = 0.25 + 0.75 * lens_window.astype(jnp.float32)
    source = wave_spectrum * weight
    gain_rate = (diffraction_gain / orders)[:, None, None]
    widened = extended(source, (("tx", 2), ("ty", 3)), 4)
    inside = inside_grid(height, breadth, 4)
    advanced = widened
    for offset, scale_divider in ((1, 4.0), (2, 3.0), (3, 2.0), (4, 1.0)):
        bending = gain_rate * laplace(advanced)
        anchor = widened[
            :, :, offset : widened.shape[2] - offset, offset : widened.shape[3] - offset
        ]
        retain = inside[offset : inside.shape[0] - offset, offset : inside.shape[1] - offset]
        advanced = (anchor + 1.0 / scale_divider * jnp.stack([-bending[1], bending[0]])) * retain
    dft_table = build_table(overall)
    scale_synth = overall ** (-0.5)
    scale_analysis = 2.0 * math.sqrt(overall) / CYCLE_READINGS
    all_orders = jnp.arange(1, overall + 1, dtype=jnp.int32).astype(jnp.float32)
    rate = nonlinear_gain / overall * all_orders[:, None]
    pixels = lax.all_to_all(advanced, HARM, split_axis=2, concat_axis=1, tiled=True)
    block_rows = pixels.shape[2]
    block_cols = pixels.shape[3]
    stacked = pixels.reshape(2 * overall, block_rows * block_cols)
    pressure = scale_synth * jnp.dot(dft_table, stacked, precision=lax.Precision.HIGHEST)
    spectrum = scale_analysis * lax.dot_general(
        dft_table, pressure * pressure, (((0,), (0,)), ((), ())), precision=lax.Precision.HIGHEST
    )
    real_new = stacked[:overall] - rate * spectrum[overall:]
    imag_new = stacked[overall:] + rate * spectrum[:overall]
    updated = jnp.stack([real_new, imag_new]).reshape(2, overall, block_rows, block_cols)
    updated, real_new, imag_new = (updated, real_new, imag_new)
    heat_per_pixel = jnp.sum(
        all_orders[:, None] * (real_new * real_new + imag_new * imag_new), axis=0
    )
    field_out = lax.all_to_all(updated, HARM, split_axis=1, concat_axis=2, tiled=True)
    heat_tile = gather_axes(
        heat_per_pixel.reshape(1, 1, pixels.shape[2], pixels.shape[3]), HARM, (0, 1), 2
    )[0, 0]
    codes = jnp.arange(attenuation_by_kind.shape[0], dtype=jnp.int32)
    onehot = (medium_label[None, :, :] == codes[:, None, None]).astype(jnp.float32)
    absorb_map = jnp.sum(attenuation_by_kind[:, None, None] * onehot, axis=0)
    conduct_map = jnp.sum(diffusivity_by_kind[:, None, None] * onehot, axis=0)
    perfuse_map = jnp.sum(blood_drain_by_kind[:, None, None] * onehot, axis=0)
    deposit = absorb_map * heat_tile / (overall * overall)
    bundle = jnp.stack([thermal_excess_prior, deposit, conduct_map, perfuse_map])
    wide_bundle = extended(bundle, (("tx", 1), ("ty", 2)), 4)
    thermal_excess_later = wide_bundle[0]
    for offset in (1, 2, 3, 4):
        inner = wide_bundle[
            :, offset : wide_bundle.shape[1] - offset, offset : wide_bundle.shape[2] - offset
        ]
        center = thermal_excess_later[1:-1, 1:-1]
        thermal_excess_later = (
            center + inner[2] * laplace(thermal_excess_later) - inner[3] * center + inner[1]
        )
    return (field_out, thermal_excess_later)


def solution(mesh):
    split = Mesh(
        mesh.devices.reshape(2, 2, mesh.shape["tx"], mesh.shape["ty"]),
        ("harm_0", "harm_1", "tx", "ty"),
    )
    in_specs = (
        P(None, HARM, "tx", "ty"),
        P("tx", "ty"),
        P("tx", "ty"),
        P("tx", "ty"),
        P(),
        P(),
        P(),
    )
    out_specs = (P(None, HARM, "tx", "ty"), P("tx", "ty"))
    return jax.shard_map(body, mesh=split, in_specs=in_specs, out_specs=out_specs, check_vma=False)
```

profile of v0, /device:TPU:57, one launch (start us, length us, event | category | flops | bytes accessed | tf_op | source)
XLA Modules:
  0.0 163.6 jit_solution(6992596038649293184)
XLA Ops:
  0.6 1.2 copy.26
  1.9 0.7 multiply_add_fusion
  2.6 0.1 broadcast_multiply_fusion
  2.7 3.1 %collective-permute-start = (f32[2,128,4,128]{1,3,2,0:T(8,128)S(1)}, f32[2,128,4,128]{1,3,2,0:T(8,128)S(1)}, u32[]{:S(2)}, u32[]{:S(2)}) collective-permute-start(f32[2,128,4,128]{1,3,2,0:T(8,128)S(1)} %broadcast_multiply_fusion), channel_id=1, source_target_pairs={{0,8},{8,16},{16,24},{24,32},{32,40},{40,48},{48,56},{56,64},{64,7... | collective-permute-start | bytes 1572872 | tf_op jit(solution)/shard_map/ppermute | solution.py:22
  5.8 4.3 %collective-permute-start.1 = (f32[2,128,4,128]{1,3,2,0:T(8,128)S(1)}, f32[2,128,4,128]{1,3,2,0:T(8,128)S(1)}, u32[]{:S(2)}, u32[]{:S(2)}) collective-permute-start(f32[2,128,4,128]{1,3,2,0:T(8,128)S(1)} %broadcast_multiply_fusion), channel_id=1, source_target_pairs={{8,0},{16,8},{24,16},{32,24},{40,32},{48,40},{56,48},{64,56},{72,6... | collective-permute-start | bytes 1572872 | tf_op jit(solution)/shard_map/ppermute | solution.py:25
  10.1 0.1 and_convert_fusion
  10.2 9.3 %collective-permute-done = f32[2,128,4,128]{1,3,2,0:T(8,128)S(1)} collective-permute-done((f32[2,128,4,128]{1,3,2,0:T(8,128)S(1)}, f32[2,128,4,128]{1,3,2,0:T(8,128)S(1)}, u32[]{:S(2)}, u32[]{:S(2)}) %collective-permute-start) | collective-permute-done | bytes 524320 | tf_op jit(solution)/shard_map/ppermute | solution.py:22
  19.5 0.9 collective-permute-done.1
  20.4 3.5 %collective-permute-start.2 = (f32[2,128,12,4]{1,3,2,0:T(4,128)S(1)}, f32[2,128,12,4]{1,3,2,0:T(4,128)S(1)}, u32[]{:S(2)}, u32[]{:S(2)}) collective-permute-start(f32[2,128,12,4]{1,3,2,0:T(4,128)S(1)} %get-tuple-element.8), channel_id=1, source_target_pairs={{0,1},{1,2},{2,3},{3,4},{4,5},{5,6},{6,7},{8,9},{9,10},{10,11},{11... | collective-permute-start | bytes 147464 | tf_op jit(solution)/shard_map/ppermute | solution.py:22
  24.0 1.9 %collective-permute-start.3 = (f32[2,128,12,4]{1,3,2,0:T(4,128)S(1)}, f32[2,128,12,4]{1,3,2,0:T(4,128)S(1)}, u32[]{:S(2)}, u32[]{:S(2)}) collective-permute-start(f32[2,128,12,4]{1,3,2,0:T(4,128)S(1)} %get-tuple-element.9), channel_id=1, source_target_pairs={{1,0},{2,1},{3,2},{4,3},{5,4},{6,5},{7,6},{9,8},{10,9},{11,10},{12... | collective-permute-start | bytes 147464 | tf_op jit(solution)/shard_map/ppermute | solution.py:25
  25.9 0.1 slice.322
  26.0 0.1 slice.330
  26.1 0.1 slice.338
  26.2 0.1 slice.346
  26.2 0.0 collective-permute-done.2
  26.2 2.8 %collective-permute-done.3 = f32[2,128,12,4]{1,3,2,0:T(4,128)S(1)} collective-permute-done((f32[2,128,12,4]{1,3,2,0:T(4,128)S(1)}, f32[2,128,12,4]{1,3,2,0:T(4,128)S(1)}, u32[]{:S(2)}, u32[]{:S(2)}) %collective-permute-start.3) | collective-permute-done | bytes 49184 | tf_op jit(solution)/shard_map/ppermute | solution.py:25
  29.0 0.2 pad_maximum_fusion.7
  29.2 0.5 fusion.12
  29.6 0.1 slice_negate_fusion
  29.7 0.3 fusion.14
  30.1 0.4 fusion.17
  30.4 0.1 slice_negate_fusion.1
  30.5 0.3 fusion.18
  30.8 0.3 fusion.20
  31.1 0.1 slice_negate_fusion.2
  31.2 0.2 fusion.21
  31.4 0.2 fusion.23
  31.6 0.2 fusion.24
  31.8 0.0 copy-start.3
  31.9 0.0 copy-start.4
  31.9 0.0 copy-start.5
  31.9 0.0 copy-start.6
  31.9 1.0 copy.27
  32.9 16.3 %all-to-all-start = ((f32[2,128,4,128]{3,1,0,2:T(8,128)}), f32[2,128,4,128]{3,1,0,2:T(8,128)S(1)}, u32[]{:S(2)}, u32[]{:S(2)}) async-start(f32[2,128,4,128]{3,1,0,2:T(8,128)} %copy.27), calls=%async_computation | async-start | bytes 1048576 | tf_op jit(solution)/shard_map/all_to_all | solution.py:115
  49.2 0.0 copy-done.3
  49.2 0.0 copy-done.4
  49.3 0.0 copy-done.5
  49.3 0.1 select_reduce_fusion.2
  49.4 18.1 %fusion.10 = (f32[2048,512]{1,0:T(8,128)}, f32[2048,512]{1,0:T(8,128)}) fusion(s32[512]{0:T(512)S(1)} %iota_add_fusion), kind=kLoop, calls=%fused_computation.15 | loop fusion | flops 15728640 | bytes 8390656 | tf_op jit(solution)/shard_map/cos | solution.py:66
  67.4 15.2 %all-to-all-done = f32[2,128,4,128]{3,1,0,2:T(8,128)S(1)} async-done(((f32[2,128,4,128]{3,1,0,2:T(8,128)}), f32[2,128,4,128]{3,1,0,2:T(8,128)S(1)}, u32[]{:S(2)}, u32[]{:S(2)}) %all-to-all-start) | async-done | bytes 524320 | tf_op jit(solution)/shard_map/all_to_all | solution.py:115
  82.7 9.8 %fusion.9 = f32[2048,128]{1,0:T(8,128)S(1)} fusion(f32[1024,128]{1,0:T(8,128)S(1)} %bitcast.92, f32[2048,512]{1,0:T(8,128)} %get-tuple-element.25, f32[2048,512]{1,0:T(8,128)} %get-tuple-element.24), kind=kOutput, calls=%fused_computation.14 | convolution fusion | flops 3223846912 | bytes 9961472 | tf_op jit(solution)/shard_map/dot_general | solution.py:119
  92.5 13.1 %fusion.15 = f32[1024,128]{1,0:T(8,128)S(1)} fusion(f32[2048,128]{1,0:T(8,128)S(1)} %fusion.9, f32[2048,512]{1,0:T(8,128)S(1)} %copy-done.1, f32[2048,512]{1,0:T(8,128)S(1)} %copy-done), kind=kOutput, calls=%fused_computation.25 | convolution fusion | flops 3223453696 | bytes 9961472 | tf_op jit(solution)/shard_map/dot_general | solution.py:120
  105.6 0.0 copy-start.2
  105.7 0.2 multiply_reduce_fusion
  105.9 11.8 %all-gather.2 = f32[2,1,128]{2,1,0:T(1,128)S(1)} all-gather(f32[1,1,128]{2,1,0:T(1,128)S(1)} %bitcast.111), channel_id=2, replica_groups=mesh['harm_0'=2,'harm_1'=2,'tx'=16,'ty'=8] {'harm_0'}, dimensions={0}, use_global_device_ids=true | all-gather | bytes 1536 | tf_op jit(solution)/shard_map/all_gather | solution.py:39
  117.7 3.6 %all-gather.1 = f32[4,1,1,1,128]{4,3,2,1,0:T(1,128)S(1)} all-gather(f32[2,1,1,1,128]{4,3,2,1,0:T(1,128)S(1)} %bitcast.110), channel_id=3, replica_groups=mesh['harm_0'=2,'harm_1'=2,'tx'=16,'ty'=8] {'harm_1'}, dimensions={0}, use_global_device_ids=true | all-gather | bytes 3072 | tf_op jit(solution)/shard_map/all_gather | solution.py:39
  121.3 3.0 %collective-permute-start.4 = (f32[4,4,128]{2,1,0:T(4,128)S(1)}, f32[4,4,128]{2,1,0:T(4,128)S(1)}, u32[]{:S(2)}, u32[]{:S(2)}) collective-permute-start(f32[4,4,128]{2,1,0:T(4,128)S(1)} %pad_maximum_fusion.15), channel_id=1, source_target_pairs={{0,8},{8,16},{16,24},{24,32},{32,40},{40,48},{48,56},{56,64},{64,7... | collective-permute-start | bytes 24584 | tf_op jit(solution)/shard_map/ppermute | solution.py:22
  124.3 5.2 %collective-permute-start.5 = (f32[4,4,128]{2,1,0:T(4,128)S(1)}, f32[4,4,128]{2,1,0:T(4,128)S(1)}, u32[]{:S(2)}, u32[]{:S(2)}) collective-permute-start(f32[4,4,128]{2,1,0:T(4,128)S(1)} %pad_maximum_fusion.15), channel_id=1, source_target_pairs={{8,0},{16,8},{24,16},{32,24},{40,32},{48,40},{56,48},{64,56},{72,6... | collective-permute-start | bytes 24584 | tf_op jit(solution)/shard_map/ppermute | solution.py:25
  129.5 1.2 copy.29
  130.7 4.1 %all-to-all-start.1 = ((f32[2,512,1,128]{3,0,2,1:T(2,128)}), f32[2,512,1,128]{3,0,2,1:T(2,128)S(1)}, u32[]{:S(2)}, u32[]{:S(2)}) async-start(f32[2,512,1,128]{3,0,2,1:T(2,128)} %copy.29), calls=%async_computation.1 | async-start | bytes 1048576 | tf_op jit(solution)/shard_map/all_to_all | solution.py:130
  134.8 0.0 collective-permute-done.4
  134.8 0.0 collective-permute-done.5
  134.8 0.1 fusion.57
  134.9 1.9 %collective-permute-start.6 = (f32[4,12,4]{2,1,0:T(8,128)S(1)}, f32[4,12,4]{2,1,0:T(8,128)S(1)}, u32[]{:S(2)}, u32[]{:S(2)}) collective-permute-start(f32[4,12,4]{2,1,0:T(8,128)S(1)} %get-tuple-element.22), channel_id=1, source_target_pairs={{0,1},{1,2},{2,3},{3,4},{4,5},{5,6},{6,7},{8,9},{9,10},{10,11},{11... | collective-permute-start | bytes 2312 | tf_op jit(solution)/shard_map/ppermute | solution.py:22
  136.8 3.4 %collective-permute-start.7 = (f32[4,12,4]{2,1,0:T(8,128)S(1)}, f32[4,12,4]{2,1,0:T(8,128)S(1)}, u32[]{:S(2)}, u32[]{:S(2)}) collective-permute-start(f32[4,12,4]{2,1,0:T(8,128)S(1)} %get-tuple-element.23), channel_id=1, source_target_pairs={{1,0},{2,1},{3,2},{4,3},{5,4},{6,5},{7,6},{9,8},{10,9},{11,10},{12... | collective-permute-start | bytes 2312 | tf_op jit(solution)/shard_map/ppermute | solution.py:25
  140.2 0.0 collective-permute-done.6
  140.2 12.3 %collective-permute-done.7 = f32[4,12,4]{2,1,0:T(8,128)S(1)} collective-permute-done((f32[4,12,4]{2,1,0:T(8,128)S(1)}, f32[4,12,4]{2,1,0:T(8,128)S(1)}, u32[]{:S(2)}, u32[]{:S(2)}) %collective-permute-start.7) | collective-permute-done | bytes 800 | tf_op jit(solution)/shard_map/ppermute | solution.py:25
  152.5 0.1 pad_maximum_fusion.10
  152.7 0.1 fusion.27
  152.8 0.1 fusion.39
  152.9 0.1 fusion.33
  152.9 0.7 fusion.49
  153.6 8.8 %all-to-all-done.1 = f32[2,512,1,128]{3,0,2,1:T(2,128)S(1)} async-done(((f32[2,512,1,128]{3,0,2,1:T(2,128)}), f32[2,512,1,128]{3,0,2,1:T(2,128)S(1)}, u32[]{:S(2)}, u32[]{:S(2)}) %all-to-all-start.1) | async-done | bytes 524320 | tf_op jit(solution)/shard_map/all_to_all | solution.py:130
  162.4 1.1 copy.36
  (22 shorter events, 0.2 us)
Async XLA Ops:
  2.7 16.8 %collective-permute-start = (f32[2,128,4,128]{1,3,2,0:T(8,128)S(1)}, f32[2,128,4,128]{1,3,2,0:T(8,128)S(1)}, u32[]{:S(2)}, u32[]{:S(2)}) collective-permute-start(f32[2,128,4,128]{1,3,2,0:T(8,128)S(1)} %broadcast_multiply_fusion), channel_id=1, source_target_pairs={{0,8},{8,16},{16,24},{24,32},{32,40},{40,48},{48,56},{56,64},{64,7... | collective-permute-start | bytes 1572872 | tf_op jit(solution)/shard_map/ppermute | solution.py:22
  5.8 14.6 %collective-permute-start.1 = (f32[2,128,4,128]{1,3,2,0:T(8,128)S(1)}, f32[2,128,4,128]{1,3,2,0:T(8,128)S(1)}, u32[]{:S(2)}, u32[]{:S(2)}) collective-permute-start(f32[2,128,4,128]{1,3,2,0:T(8,128)S(1)} %broadcast_multiply_fusion), channel_id=1, source_target_pairs={{8,0},{16,8},{24,16},{32,24},{40,32},{48,40},{56,48},{64,56},{72,6... | collective-permute-start | bytes 1572872 | tf_op jit(solution)/shard_map/ppermute | solution.py:25
  20.4 5.8 %collective-permute-start.2 = (f32[2,128,12,4]{1,3,2,0:T(4,128)S(1)}, f32[2,128,12,4]{1,3,2,0:T(4,128)S(1)}, u32[]{:S(2)}, u32[]{:S(2)}) collective-permute-start(f32[2,128,12,4]{1,3,2,0:T(4,128)S(1)} %get-tuple-element.8), channel_id=1, source_target_pairs={{0,1},{1,2},{2,3},{3,4},{4,5},{5,6},{6,7},{8,9},{9,10},{10,11},{11... | collective-permute-start | bytes 147464 | tf_op jit(solution)/shard_map/ppermute | solution.py:22
  24.0 5.0 %collective-permute-start.3 = (f32[2,128,12,4]{1,3,2,0:T(4,128)S(1)}, f32[2,128,12,4]{1,3,2,0:T(4,128)S(1)}, u32[]{:S(2)}, u32[]{:S(2)}) collective-permute-start(f32[2,128,12,4]{1,3,2,0:T(4,128)S(1)} %get-tuple-element.9), channel_id=1, source_target_pairs={{1,0},{2,1},{3,2},{4,3},{5,4},{6,5},{7,6},{9,8},{10,9},{11,10},{12... | collective-permute-start | bytes 147464 | tf_op jit(solution)/shard_map/ppermute | solution.py:25
  31.8 17.4 %copy-start.3 = (s32[4,128]{1,0:T(4,128)S(1)}, s32[4,128]{1,0:T(4,128)}, u32[]{:S(2)}) copy-start(s32[4,128]{1,0:T(4,128)} %param.9) | copy-start | bytes 6148
  31.9 17.4 %copy-start.4 = (f32[8]{0:T(128)S(1)}, f32[8]{0:T(128)}, u32[]{:S(2)}) copy-start(f32[8]{0:T(128)} %param.11) | copy-start | bytes 100
  31.9 17.4 %copy-start.5 = (f32[8]{0:T(128)S(1)}, f32[8]{0:T(128)}, u32[]{:S(2)}) copy-start(f32[8]{0:T(128)} %param.12) | copy-start | bytes 100
  31.9 17.4 %copy-start.6 = (f32[8]{0:T(128)S(1)}, f32[8]{0:T(128)}, u32[]{:S(2)}) copy-start(f32[8]{0:T(128)} %param.13) | copy-start | bytes 100
  32.9 49.8 %all-to-all-start = ((f32[2,128,4,128]{3,1,0,2:T(8,128)}), f32[2,128,4,128]{3,1,0,2:T(8,128)S(1)}, u32[]{:S(2)}, u32[]{:S(2)}) async-start(f32[2,128,4,128]{3,1,0,2:T(8,128)} %copy.27), calls=%async_computation | async-start | bytes 1048576 | tf_op jit(solution)/shard_map/all_to_all | solution.py:115
  82.7 9.8 %copy-start = (f32[2048,512]{1,0:T(8,128)S(1)}, f32[2048,512]{1,0:T(8,128)}, u32[]{:S(2)}) copy-start(f32[2048,512]{1,0:T(8,128)} %get-tuple-element.24) | copy-start | bytes 12582916
  82.7 9.8 %copy-start.1 = (f32[2048,512]{1,0:T(8,128)S(1)}, f32[2048,512]{1,0:T(8,128)}, u32[]{:S(2)}) copy-start(f32[2048,512]{1,0:T(8,128)} %get-tuple-element.25) | copy-start | bytes 12582916
  105.6 15.7 %copy-start.2 = (f32[4,128]{1,0:T(4,128)S(1)}, f32[4,128]{1,0:T(4,128)}, u32[]{:S(2)}) copy-start(f32[4,128]{1,0:T(4,128)} %param.10) | copy-start | bytes 6148
  121.3 13.5 %collective-permute-start.4 = (f32[4,4,128]{2,1,0:T(4,128)S(1)}, f32[4,4,128]{2,1,0:T(4,128)S(1)}, u32[]{:S(2)}, u32[]{:S(2)}) collective-permute-start(f32[4,4,128]{2,1,0:T(4,128)S(1)} %pad_maximum_fusion.15), channel_id=1, source_target_pairs={{0,8},{8,16},{16,24},{24,32},{32,40},{40,48},{48,56},{56,64},{64,7... | collective-permute-start | bytes 24584 | tf_op jit(solution)/shard_map/ppermute | solution.py:22
  124.3 10.5 %collective-permute-start.5 = (f32[4,4,128]{2,1,0:T(4,128)S(1)}, f32[4,4,128]{2,1,0:T(4,128)S(1)}, u32[]{:S(2)}, u32[]{:S(2)}) collective-permute-start(f32[4,4,128]{2,1,0:T(4,128)S(1)} %pad_maximum_fusion.15), channel_id=1, source_target_pairs={{8,0},{16,8},{24,16},{32,24},{40,32},{48,40},{56,48},{64,56},{72,6... | collective-permute-start | bytes 24584 | tf_op jit(solution)/shard_map/ppermute | solution.py:25
  130.7 31.7 %all-to-all-start.1 = ((f32[2,512,1,128]{3,0,2,1:T(2,128)}), f32[2,512,1,128]{3,0,2,1:T(2,128)S(1)}, u32[]{:S(2)}, u32[]{:S(2)}) async-start(f32[2,512,1,128]{3,0,2,1:T(2,128)} %copy.29), calls=%async_computation.1 | async-start | bytes 1048576 | tf_op jit(solution)/shard_map/all_to_all | solution.py:130
  134.9 5.3 %collective-permute-start.6 = (f32[4,12,4]{2,1,0:T(8,128)S(1)}, f32[4,12,4]{2,1,0:T(8,128)S(1)}, u32[]{:S(2)}, u32[]{:S(2)}) collective-permute-start(f32[4,12,4]{2,1,0:T(8,128)S(1)} %get-tuple-element.22), channel_id=1, source_target_pairs={{0,1},{1,2},{2,3},{3,4},{4,5},{5,6},{6,7},{8,9},{9,10},{10,11},{11... | collective-permute-start | bytes 2312 | tf_op jit(solution)/shard_map/ppermute | solution.py:22
  136.8 15.7 %collective-permute-start.7 = (f32[4,12,4]{2,1,0:T(8,128)S(1)}, f32[4,12,4]{2,1,0:T(8,128)S(1)}, u32[]{:S(2)}, u32[]{:S(2)}) collective-permute-start(f32[4,12,4]{2,1,0:T(8,128)S(1)} %get-tuple-element.23), channel_id=1, source_target_pairs={{1,0},{2,1},{3,2},{4,3},{5,4},{6,5},{7,6},{9,8},{10,9},{11,10},{12... | collective-permute-start | bytes 2312 | tf_op jit(solution)/shard_map/ppermute | solution.py:25
where the time goes:
time: 164 us
  waiting for transfers between devices  49.4 us (30%)
  starting transfers between devices  46.7 us (28%)
  other arithmetic  23.2 us (14%)
  matrix products  22.9 us (14%)
  blocking collectives  15.4 us (9%)
  local copies, waits for them, and re-layouts  5.04 us (3%)
    cos x1, other arithmetic, build_table(): return jnp.concatenate([jnp.cos(angle), -jnp.sin(angle)], axis=1)  18.1 us
    all_to_all x1, starting transfers between devices, body(): lax.all_to_all(advanced, HARM, split_axis=2, concat_axis=1, tiled=True)  16.3 us
    ppermute x4, waiting for transfers between devices, extended(): lax.ppermute(lax.slice_in_dim(block, 0, width, axis=dim), axis, backward)  16 us
    all_gather x2, blocking collectives, all_blocks(): pieces = lax.all_gather(pieces, axes[k])  15.4 us
    all_to_all x1, waiting for transfers between devices, body(): lax.all_to_all(advanced, HARM, split_axis=2, concat_axis=1, tiled=True)  15.2 us
    ppermute x4, starting transfers between devices, extended(): lax.ppermute(lax.slice_in_dim(block, 0, width, axis=dim), axis, backward)  14.7 us
    dot_general x1, matrix products, body(): lax.dot_general(dft_table, pressure * pressure, (((0,), (0,)), ((), ())),...  13.1 us
    ppermute x4, starting transfers between devices, extended(): lax.ppermute(lax.slice_in_dim(block, block.shape[dim] - width, None, axis...  11.5 us
  transfers between devices with their start and end apart: 10, of which 6 were waited for; matrix products, arithmetic and copies ran while one was open for 13% of the time, Pallas kernels for 0%

commit v1 on v0

v1 whole, which is shorter than its diff:
```python
import math

import jax
import jax.numpy as jnp
import numpy as np
from jax import lax
from jax.experimental import pallas as pl
from jax.experimental.pallas import tpu as pltpu
from jax.sharding import PartitionSpec as P

CYCLE_READINGS = 2048
HALF = CYCLE_READINGS // 2
HARMONICS = 512
OWN = 128
ROWS = 4
COLS = 128
CHUNKS = 4
WIDTH = COLS // CHUNKS
PAD = 16
F32 = jnp.float32
BF16 = jnp.bfloat16

diffraction_gain = 0.3
nonlinear_gain = 0.3

TX = 16
TY = 8
AROUND = [(dy, dx) for dy in (-1, 0, 1) for dx in (-1, 0, 1) if (dy, dx) != (0, 0)]


def trig(product, period):
    angle = 2.0 * np.pi * (product % period) / period
    return np.cos(angle).astype(np.float32), np.sin(angle).astype(np.float32)


def table_factors():
    n = np.arange(1, HARMONICS + 1, dtype=np.int64)
    fine_c, fine_s = trig(n[:, None] * (2 * np.arange(128)[None, :] + 1), 2 * CYCLE_READINGS)
    coarse_c, coarse_s = trig(np.arange(8)[:, None] * np.arange(1, 17)[None, :], 16)
    coarse_c = np.repeat(coarse_c[:, :, None], 128, axis=2)
    coarse_s = np.repeat(coarse_s[:, :, None], 128, axis=2)
    far_c, far_s = trig(np.arange(64)[:, None] * n[None, :], 128)
    near_c, near_s = trig((2 * np.arange(16)[:, None] + 1) * n[None, :], 2 * CYCLE_READINGS)
    return fine_c, fine_s, coarse_c, coarse_s, far_c, far_s, near_c, near_s


def split(x):
    high = x.astype(BF16)
    return high, (x - high.astype(F32)).astype(BF16)


def product(x, high_table, low_table):
    m = x.shape[0]
    high, low = split(x)
    both = jnp.dot(jnp.concatenate([high, low], axis=0), high_table, preferred_element_type=F32)
    return both[:m] + both[m:] + jnp.dot(high, low_table, preferred_element_type=F32)


def kernel(
    src, label, prior, attenuation, drain, diffusivity,
    fine_c, fine_s, coarse_c, coarse_s, far_c, far_s, near_c, near_s,
    field, later,
    S, VA, VB, M, R, Y, W,
    synth_c, synth_s, anal_c, anal_s,
    factors_fine, factors_coarse, factors_far, factors_near,
    early, late, heat_rows, heat_out, wide,
    load_sem, row_send, row_recv, col_send, col_recv, corner_send, corner_recv,
    early_send, early_recv, late_send, late_recv,
    one_send, one_recv, two_send, two_recv, heat_send, heat_recv,
):
    harm = lax.axis_index("harm")
    tx = lax.axis_index("tx")
    ty = lax.axis_index("ty")
    half = harm // 2
    core = harm % 2
    far_ty = (ty + 4) % TY
    wrapped = (ty + 4) // TY

    def remote(a, b, send, recv, device):
        return pltpu.make_async_remote_copy(
            src_ref=a, dst_ref=b, send_sem=send, recv_sem=recv,
            device_id=device, device_id_type=pl.DeviceIdType.MESH,
        )

    def owner(row):
        return (2 * ((row // 2 + wrapped) % 2) + row % 2, tx, far_ty)

    own_row = 2 * ((half + (far_ty + 4) // TY) % 2) + core

    def inside(dy, dx):
        ok = None
        for at, step, count in ((tx, dy, TX), (ty, dx, TY)):
            if step == 0:
                continue
            one = at > 0 if step < 0 else at < count - 1
            ok = one if ok is None else jnp.logical_and(ok, one)
        return ok

    loads = []
    for i, (a, b) in enumerate((
        (fine_c, factors_fine.at[0]), (fine_s, factors_fine.at[1]),
        (coarse_c, factors_coarse.at[0]), (coarse_s, factors_coarse.at[1]),
        (far_c, factors_far.at[0]), (far_s, factors_far.at[1]),
        (near_c, factors_near.at[0]), (near_s, factors_near.at[1]),
    )):
        copy = pltpu.make_async_copy(a, b, load_sem.at[i])
        copy.start()
        loads.append(copy)

    @pl.when(tx == 0)
    def _():
        S[:, 0:4] = jnp.zeros((2, 4, COLS + 2 * PAD, OWN), F32)
        for dx in range(3):
            early[0, dx] = jnp.zeros((3, ROWS, COLS), F32)
            late[0, dx] = jnp.zeros((ROWS, COLS), F32)

    @pl.when(tx == TX - 1)
    def _():
        S[:, 8:12] = jnp.zeros((2, 4, COLS + 2 * PAD, OWN), F32)
        for dx in range(3):
            early[2, dx] = jnp.zeros((3, ROWS, COLS), F32)
            late[2, dx] = jnp.zeros((ROWS, COLS), F32)

    @pl.when(ty == 0)
    def _():
        S[:, :, 8:16] = jnp.zeros((2, 12, 8, OWN), F32)
        for dy in range(3):
            early[dy, 0] = jnp.zeros((3, ROWS, COLS), F32)
            late[dy, 0] = jnp.zeros((ROWS, COLS), F32)

    @pl.when(ty == TY - 1)
    def _():
        S[:, :, PAD + COLS:PAD + COLS + 8] = jnp.zeros((2, 12, 8, OWN), F32)
        for dy in range(3):
            early[dy, 2] = jnp.zeros((3, ROWS, COLS), F32)
            late[dy, 2] = jnp.zeros((ROWS, COLS), F32)

    barrier = pltpu.get_barrier_semaphore()
    for dy, dx in AROUND:
        @pl.when(inside(dy, dx))
        def _():
            pl.semaphore_signal(barrier, inc=1, device_id=(harm, tx + dy, ty + dx), device_id_type=pl.DeviceIdType.MESH)
    for j in range(4):
        pl.semaphore_signal(barrier, inc=1, device_id=(j, tx, far_ty), device_id_type=pl.DeviceIdType.MESH)

    kinds = label[...]
    conduct = jnp.zeros((ROWS, COLS), F32)
    perfuse = jnp.zeros((ROWS, COLS), F32)
    absorb = jnp.zeros((ROWS, COLS), F32)
    for k in range(8):
        hit = kinds == k
        conduct = jnp.where(hit, diffusivity[k], conduct)
        perfuse = jnp.where(hit, drain[k], perfuse)
        absorb = jnp.where(hit, attenuation[k], absorb)
    early[1, 1, 0] = prior[...]
    early[1, 1, 1] = conduct
    early[1, 1, 2] = perfuse

    def edges(at, count):
        return jnp.where(at == 0, 1, 0) + jnp.where(at == count - 1, 1, 0)

    pl.semaphore_wait(barrier, (3 - edges(tx, TX)) * (3 - edges(ty, TY)) + 3)

    def row_copy(side, c):
        return remote(
            src.at[:, :, pl.ds(c * WIDTH, WIDTH), :],
            S.at[:, pl.ds(8 * side, 4), pl.ds(PAD + c * WIDTH, WIDTH), :],
            row_send.at[side, c], row_recv.at[side, c], (harm, tx + 1 - 2 * side, ty),
        )

    def col_copy(side):
        return remote(
            src.at[:, :, pl.ds(0 if side else COLS - 8, 8), :],
            S.at[:, 4:8, pl.ds(PAD + COLS if side else PAD - 8, 8), :],
            col_send.at[side], col_recv.at[side], (harm, tx, ty + 1 - 2 * side),
        )

    def corner_copy(side, vertical):
        at = PAD + COLS if side else PAD - 8
        return remote(
            S.at[:, 4:8, pl.ds(at, 8), :],
            S.at[:, pl.ds(8 * vertical, 4), pl.ds(at, 8), :],
            corner_send.at[side, vertical], corner_recv.at[side, vertical],
            (harm, tx + 1 - 2 * vertical, ty),
        )

    def to_side(side):
        return tx < TX - 1 if side == 0 else tx > 0

    def from_side(side):
        return tx > 0 if side == 0 else tx < TX - 1

    def to_col(side):
        return ty < TY - 1 if side == 0 else ty > 0

    def from_col(side):
        return ty > 0 if side == 0 else ty < TY - 1

    for side in (0, 1):
        @pl.when(to_col(side))
        def _():
            col_copy(side).start()
    for c in range(CHUNKS):
        for side in (0, 1):
            @pl.when(to_side(side))
            def _():
                row_copy(side, c).start()

    def early_copy(dy, dx):
        slot = 3 * (dy + 1) + dx + 1
        return remote(
            early.at[1, 1], early.at[1 - dy, 1 - dx], early_send.at[slot], early_recv.at[8 - slot],
            (harm, tx + dy, ty + dx),
        )

    def late_copy(dy, dx):
        slot = 3 * (dy + 1) + dx + 1
        return remote(
            late.at[1, 1], late.at[1 - dy, 1 - dx], late_send.at[slot], late_recv.at[8 - slot],
            (harm, tx + dy, ty + dx),
        )

    for dy, dx in AROUND:
        @pl.when(inside(dy, dx))
        def _():
            early_copy(dy, dx).start()

    for p in range(2):
        for row in range(ROWS):
            S[p, 4 + row, PAD:PAD + COLS, :] = src[p, row]

    lane = lax.broadcasted_iota(jnp.int32, (1, OWN), 1)
    gain = diffraction_gain / (harm * OWN + lane + 1).astype(F32)

    def row_inside(row):
        at = tx * ROWS + row - 4
        return jnp.where(jnp.logical_and(at >= 0, at < TX * ROWS), 1.0, 0.0).astype(F32)

    def stencil(c):
        base = c * WIDTH
        for k, source, target in ((1, S, VA), (2, VA, VB), (3, VB, VA), (4, VA, M)):
            low, count = (PAD, WIDTH) if k == 4 else (8, WIDTH + 16)
            shift = base if k == 1 else 0
            at = ty * COLS + base + low - PAD + lax.broadcasted_iota(jnp.int32, (count, OWN), 0)
            valid = jnp.logical_and(at >= 0, at < TY * COLS)
            g = jnp.where(valid, gain * (1.0 / (5 - k)), 0.0)

            def one_row(row, carry):
                gr = g * row_inside(row)
                laps = []
                for p in range(2):
                    center = source[p, row, pl.ds(shift + low, count), :]
                    laps.append(
                        source[p, row + 1, pl.ds(shift + low, count), :]
                        + source[p, row - 1, pl.ds(shift + low, count), :]
                        + source[p, row, pl.ds(shift + low + 1, count), :]
                        + source[p, row, pl.ds(shift + low - 1, count), :]
                        - 4.0 * center
                    )
                real = S[0, row, pl.ds(base + low, count), :] - gr * laps[1]
                imag = S[1, row, pl.ds(base + low, count), :] + gr * laps[0]
                if k == 4:
                    target[0, row - 4, pl.ds(base, count), :] = real
                    target[1, row - 4, pl.ds(base, count), :] = imag
                else:
                    target[0, row, pl.ds(low, count), :] = real
                    target[1, row, pl.ds(low, count), :] = imag
                return carry

            lax.fori_loop(k, 12 - k, one_row, 0)

    def one_copy(c, row):
        return remote(
            M.at[:, row, pl.ds(c * WIDTH, WIDTH), :],
            R.at[harm, :, pl.ds(c * WIDTH, WIDTH), :],
            one_send.at[c, row], one_recv.at[c, harm], owner(row),
        )

    def one_arrival(c, j):
        return remote(
            M.at[:, 0, pl.ds(c * WIDTH, WIDTH), :],
            R.at[j, :, pl.ds(c * WIDTH, WIDTH), :],
            one_send.at[c, 0], one_recv.at[c, j], (j, tx, far_ty),
        )

    def two_copy(c, j):
        return remote(
            Y.at[j, :, pl.ds(c * WIDTH, WIDTH), :],
            field.at[own_row, :, pl.ds(c * WIDTH, WIDTH), :],
            two_send.at[c, j], two_recv.at[c, own_row], (j, tx, far_ty),
        )

    def two_arrival(c, row):
        return remote(
            Y.at[0, :, pl.ds(c * WIDTH, WIDTH), :],
            field.at[row, :, pl.ds(c * WIDTH, WIDTH), :],
            two_send.at[c, 0], two_recv.at[c, row], owner(row),
        )

    def wait_rows(c):
        for side in (0, 1):
            @pl.when(from_side(side))
            def _():
                row_copy(side, c).wait_recv()

    def forward(side):
        @pl.when(from_col(side))
        def _():
            col_copy(side).wait_recv()
            for vertical in (0, 1):
                @pl.when(to_side(vertical))
                def _():
                    corner_copy(side, vertical).start()

    def wait_corners(side):
        @pl.when(from_col(side))
        def _():
            for vertical in (0, 1):
                @pl.when(from_side(vertical))
                def _():
                    corner_copy(side, vertical).wait_recv()

    def build_tables():
        for copy in loads:
            copy.wait()

        def by_time(i, carry):
            rows = pl.ds(pl.multiple_of(i * 16, 16), 16)
            fc = factors_fine[0, rows, :]
            fs = factors_fine[1, rows, :]
            for a in range(8):
                ac = factors_coarse[0, a]
                as_ = factors_coarse[1, a]
                for table, value in ((synth_c, ac * fc - as_ * fs), (synth_s, as_ * fc + ac * fs)):
                    high, low = split(value)
                    table[0, rows, a * 128:(a + 1) * 128] = high
                    table[1, rows, a * 128:(a + 1) * 128] = low
            return carry

        lax.fori_loop(0, HARMONICS // 16, by_time, 0)

        def by_harmonic(a, carry):
            rows = pl.ds(pl.multiple_of(a * 16, 16), 16)
            ac = factors_far[0, pl.ds(a, 1), :]
            as_ = factors_far[1, pl.ds(a, 1), :]
            nc = factors_near[0]
            ns = factors_near[1]
            for table, value in ((anal_c, ac * nc - as_ * ns), (anal_s, as_ * nc + ac * ns)):
                high, low = split(value)
                table[0, rows, :] = high
                table[1, rows, :] = low
            return carry

        lax.fori_loop(0, HALF // 16, by_harmonic, 0)

    forward(0)
    forward(1)
    wait_rows(0)
    wait_corners(0)
    for c in range(CHUNKS):
        if c + 1 < CHUNKS:
            wait_rows(c + 1)
        else:
            wait_corners(1)
        stencil(c)
        for row in range(ROWS):
            one_copy(c, row).start()
    build_tables()

    numbers = (lax.broadcasted_iota(jnp.int32, (1, HARMONICS), 1) + 1).astype(F32)
    scale = 2.0 * math.sqrt(HARMONICS) / CYCLE_READINGS / HARMONICS
    real_factor = numbers * (nonlinear_gain / HARMONICS * 4.0 * scale)
    imag_factor = numbers * (nonlinear_gain / HARMONICS * 2.0 * scale)

    def nonlinear(c, carry):
        for j in range(4):
            one_arrival(c, j).wait_recv()
        cols = pl.ds(pl.multiple_of(c * WIDTH, WIDTH), WIDTH)
        real = jnp.concatenate([R[j, 0, cols, :] for j in range(4)], axis=1)
        imag = jnp.concatenate([R[j, 1, cols, :] for j in range(4)], axis=1)
        even = product(real, synth_c[0], synth_c[1])
        odd = product(imag, synth_s[0], synth_s[1])
        cosine = product(even * even + odd * odd, anal_c[0], anal_c[1])
        sine = product(even * odd, anal_s[0], anal_s[1])
        real = real - real_factor * sine
        imag = imag + imag_factor * cosine
        weighted = numbers * (real * real + imag * imag)
        W[cols, :] = weighted[:, 0:128] + weighted[:, 128:256] + weighted[:, 256:384] + weighted[:, 384:512]
        for j in range(4):
            Y[j, 0, cols, :] = real[:, 128 * j:128 * (j + 1)]
            Y[j, 1, cols, :] = imag[:, 128 * j:128 * (j + 1)]
        for j in range(4):
            two_copy(c, j).start()
        return carry

    lax.fori_loop(0, CHUNKS, nonlinear, 0)

    heat_out[...] = lax.dot_general(
        jnp.ones((8, OWN), F32), W[...], (((1,), (1,)), ((), ())),
        precision=lax.Precision.HIGHEST, preferred_element_type=F32,
    )[0:1]

    def heat_copy(j):
        return remote(heat_out, heat_rows.at[own_row], heat_send.at[j], heat_recv.at[own_row], (j, tx, far_ty))

    for j in range(4):
        heat_copy(j).start()
    for row in range(ROWS):
        remote(heat_out, heat_rows.at[row], heat_send.at[0], heat_recv.at[row], owner(row)).wait_recv()
    for row in range(ROWS):
        late[1, 1, row:row + 1, :] = absorb[row:row + 1] * heat_rows[row] / float(HARMONICS * HARMONICS)
    for dy, dx in AROUND:
        @pl.when(inside(dy, dx))
        def _():
            late_copy(dy, dx).start()
    for dy, dx in AROUND:
        @pl.when(inside(dy, dx))
        def _():
            early_copy(-dy, -dx).wait_recv()
    for dy, dx in AROUND:
        @pl.when(inside(dy, dx))
        def _():
            late_copy(-dy, -dx).wait_recv()
    for dy in range(3):
        for dx in range(3):
            rows = slice(4 * dy, 4 * dy + 4)
            cols = slice(128 * dx, 128 * dx + 128)
            for k in range(3):
                wide[k, rows, cols] = early[dy, dx, k]
            wide[3, rows, cols] = late[dy, dx]
    for k in range(4):
        wide[k, 12:16, :] = jnp.zeros((4, 3 * COLS), F32)
    temperature = wide[0]
    wide_conduct = wide[1]
    wide_perfuse = wide[2]
    wide_deposit = wide[3]
    for _ in range(4):
        lap = (
            pltpu.roll(temperature, 15, 0) + pltpu.roll(temperature, 1, 0)
            + pltpu.roll(temperature, 3 * COLS - 1, 1) + pltpu.roll(temperature, 1, 1)
            - 4.0 * temperature
        )
        temperature = temperature + wide_conduct * lap - wide_perfuse * temperature + wide_deposit
    wide[0] = temperature
    later[...] = wide[0, 4:8, COLS:2 * COLS]

    for side in (0, 1):
        @pl.when(to_col(side))
        def _():
            col_copy(side).wait_send()
        for c in range(CHUNKS):
            @pl.when(to_side(side))
            def _():
                row_copy(side, c).wait_send()

        @pl.when(from_col(side))
        def _():
            for vertical in (0, 1):
                @pl.when(to_side(vertical))
                def _():
                    corner_copy(side, vertical).wait_send()
    for dy, dx in AROUND:
        @pl.when(inside(dy, dx))
        def _():
            early_copy(dy, dx).wait_send()
            late_copy(dy, dx).wait_send()
    for j in range(4):
        heat_copy(j).wait_send()
    for c in range(CHUNKS):
        for j in range(4):
            one_copy(c, j).wait_send()
            two_copy(c, j).wait_send()
            two_arrival(c, j).wait_recv()


def solution(mesh):
    factors = table_factors()

    def body(wave, lens, label, prior, attenuation, drain, diffusivity):
        weight = 0.25 + 0.75 * lens.astype(F32)
        src = jnp.transpose(wave * weight, (0, 2, 3, 1))
        vmem = pl.BlockSpec(memory_space=pltpu.VMEM)
        smem = pl.BlockSpec(memory_space=pltpu.SMEM)
        hbm = pl.BlockSpec(memory_space=pl.ANY)
        dma = pltpu.SemaphoreType.DMA
        field, later = pl.pallas_call(
            kernel,
            out_shape=(
                jax.ShapeDtypeStruct((ROWS, 2, COLS, OWN), F32),
                jax.ShapeDtypeStruct((ROWS, COLS), F32),
            ),
            in_specs=[vmem, vmem, vmem, smem, smem, smem] + [hbm] * 8,
            out_specs=(hbm, vmem),
            scratch_shapes=[
                pltpu.VMEM((2, 12, COLS + 2 * PAD, OWN), F32),
                pltpu.VMEM((2, 12, WIDTH + 2 * PAD, OWN), F32),
                pltpu.VMEM((2, 12, WIDTH + 2 * PAD, OWN), F32),
                pltpu.VMEM((2, ROWS, COLS, OWN), F32),
                pltpu.VMEM((4, 2, COLS, OWN), F32),
                pltpu.VMEM((4, 2, COLS, OWN), F32),
                pltpu.VMEM((COLS, OWN), F32),
                pltpu.VMEM((2, HARMONICS, HALF), BF16),
                pltpu.VMEM((2, HARMONICS, HALF), BF16),
                pltpu.VMEM((2, HALF, HARMONICS), BF16),
                pltpu.VMEM((2, HALF, HARMONICS), BF16),
                pltpu.VMEM((2, HARMONICS, 128), F32),
                pltpu.VMEM((2, 8, 16, 128), F32),
                pltpu.VMEM((2, 64, HARMONICS), F32),
                pltpu.VMEM((2, 16, HARMONICS), F32),
                pltpu.VMEM((3, 3, 3, ROWS, COLS), F32),
                pltpu.VMEM((3, 3, ROWS, COLS), F32),
                pltpu.VMEM((ROWS, 1, COLS), F32),
                pltpu.VMEM((1, COLS), F32),
                pltpu.VMEM((4, 16, 3 * COLS), F32),
                dma((8,)), dma((2, CHUNKS)), dma((2, CHUNKS)), dma((2,)), dma((2,)), dma((2, 2)), dma((2, 2)),
                dma((9,)), dma((9,)), dma((9,)), dma((9,)),
                dma((CHUNKS, 4)), dma((CHUNKS, 4)), dma((CHUNKS, 4)), dma((CHUNKS, 4)), dma((4,)), dma((4,)),
            ],
            compiler_params=pltpu.CompilerParams(
                collective_id=0, has_side_effects=True, vmem_limit_bytes=48 << 20
            ),
            name="march",
        )(src, label, prior, attenuation, drain, diffusivity, *[jnp.asarray(f) for f in factors])
        return jnp.transpose(field, (1, 3, 0, 2)), later

    in_specs = (P(None, "harm", "tx", "ty"), P("tx", "ty"), P("tx", "ty"), P("tx", "ty"), P(), P(), P())
    out_specs = (P(None, "harm", "tx", "ty"), P("tx", "ty"))
    return jax.shard_map(body, mesh=mesh, in_specs=in_specs, out_specs=out_specs, check_vma=False)
```

time: 164 us -> 90 us (0.55)
  the two profiles are of different devices: /device:TPU:57 before, /device:TPU:6 now
where the time goes in v1:
time: 90 us; the launch traced here: 88.9 us
  Pallas kernels  83.6 us (93%)
  local copies, waits for them, and re-layouts  3.69 us (4%)
    pallas_call x1, Pallas kernels, body(): pl.pallas_call(kernel, out_shape=(jax.ShapeDtypeStruct((ROWS, 2, COLS, OW...  83.6 us
    unnamed x29, local copies, waits for them, and re-layouts  3.69 us

profile of v1, /device:TPU:6, one launch (start us, length us, event | category | flops | bytes accessed | tf_op | source)
XLA Modules:
  0.0 88.9 jit_solution(16449340673518554298)
XLA Ops:
  0.6 0.7 multiply_add_fusion
  1.3 1.2 %copy.17 = f32[2,128,4,128]{1,3,2,0:T(8,128)S(1)} copy(f32[2,128,4,128]{3,2,1,0:T(4,128)} %param.15) | data formatting | bytes 1048576 | tf_op args[0]
  2.6 0.0 copy-start
  2.6 0.0 copy-start.1
  2.6 0.0 copy-start.2
  2.6 0.0 copy-start.3
  2.6 0.0 copy-start.4
  2.6 0.0 copy-start.5
  2.6 0.0 copy-start.6
  2.6 0.0 copy-start.7
  2.7 0.0 copy-start.8
  2.7 0.0 copy-start.9
  2.7 0.0 copy-start.10
  2.7 0.0 copy-start.11
  2.7 0.0 copy-start.12
  2.7 0.1 multiply_bitcast_fusion.src
  2.9 0.7 copy-done
  3.5 0.1 copy-done.1
  3.6 0.0 copy-done.2
  3.6 0.0 copy-done.3
  3.7 0.0 copy-done.4
  3.7 0.0 copy-done.5
  3.7 0.0 copy-done.6
  3.7 0.0 copy-done.7
  3.7 0.0 copy-done.8
  3.7 0.0 copy-done.9
  3.7 0.0 copy-done.10
  3.7 0.0 copy-done.11
  3.7 0.0 copy-done.12
  3.7 83.6 %march.1 = (f32[4,2,128,128]{3,2,1,0:T(8,128)S(1)}, f32[4,128]{1,0:T(4,128)S(1)}) custom-call(f32[2,4,128,128]{3,2,1,0:T(8,128)S(1)} %multiply_bitcast_fusion.src, s32[4,128]{1,0:T(4,128)S(1)} %copy-done.8, f32[4,128]{1,0:T(4,128)S(1)} %copy-done.9, f32[8]{0:T(128)S(1)} %copy-done.10, f32[8]{0:T(128)S(1)} %copy-done.11, f32[8]{0:T(128)S(1)} %copy-done.12, ...), custom_call_target="tpu_custom_call" | custom-call | tf_op jit(solution)/shard_map/march/pallas_call | solution.py:486
  87.3 1.0 %copy.18 = f32[2,128,4,128]{3,2,1,0:T(4,128)} copy(f32[2,128,4,128]{1,3,0,2:T(8,128)S(1)} %bitcast.3) | data formatting | bytes 1048576
  88.3 0.6 copy.20
Async XLA Ops:
  2.6 1.0 %copy-start = (f32[512,128]{1,0:T(8,128)S(1)}, f32[512,128]{1,0:T(8,128)}, u32[]{:S(2)}) copy-start(f32[512,128]{1,0:T(8,128)} %constant.21.clone.fine_s) | copy-start | bytes 786436
  2.6 1.0 %copy-start.1 = (f32[512,128]{1,0:T(8,128)S(1)}, f32[512,128]{1,0:T(8,128)}, u32[]{:S(2)}) copy-start(f32[512,128]{1,0:T(8,128)} %constant.20.clone.fine_c) | copy-start | bytes 786436
  2.6 1.0 %copy-start.2 = (f32[64,512]{1,0:T(8,128)S(1)}, f32[64,512]{1,0:T(8,128)}, u32[]{:S(2)}) copy-start(f32[64,512]{1,0:T(8,128)} %constant.25.clone.far_s) | copy-start | bytes 393220
  2.6 1.1 %copy-start.3 = (f32[64,512]{1,0:T(8,128)S(1)}, f32[64,512]{1,0:T(8,128)}, u32[]{:S(2)}) copy-start(f32[64,512]{1,0:T(8,128)} %constant.24.clone.far_c) | copy-start | bytes 393220
  2.6 1.1 %copy-start.4 = (f32[8,16,128]{2,1,0:T(8,128)S(1)}, f32[8,16,128]{2,1,0:T(8,128)}, u32[]{:S(2)}) copy-start(f32[8,16,128]{2,1,0:T(8,128)} %constant.23.clone.coarse_s) | copy-start | bytes 196612
  2.6 1.1 %copy-start.5 = (f32[8,16,128]{2,1,0:T(8,128)S(1)}, f32[8,16,128]{2,1,0:T(8,128)}, u32[]{:S(2)}) copy-start(f32[8,16,128]{2,1,0:T(8,128)} %constant.22.clone.coarse_c) | copy-start | bytes 196612
  2.6 1.0 %copy-start.6 = (f32[16,512]{1,0:T(8,128)S(1)}, f32[16,512]{1,0:T(8,128)}, u32[]{:S(2)}) copy-start(f32[16,512]{1,0:T(8,128)} %constant.27.clone.near_s) | copy-start | bytes 98308
  2.6 1.0 %copy-start.7 = (f32[16,512]{1,0:T(8,128)S(1)}, f32[16,512]{1,0:T(8,128)}, u32[]{:S(2)}) copy-start(f32[16,512]{1,0:T(8,128)} %constant.26.clone.near_c) | copy-start | bytes 98308
  2.7 1.0 %copy-start.8 = (s32[4,128]{1,0:T(4,128)S(1)}, s32[4,128]{1,0:T(4,128)}, u32[]{:S(2)}) copy-start(s32[4,128]{1,0:T(4,128)} %label.1) | copy-start | bytes 6148
  2.7 1.0 %copy-start.9 = (f32[4,128]{1,0:T(4,128)S(1)}, f32[4,128]{1,0:T(4,128)}, u32[]{:S(2)}) copy-start(f32[4,128]{1,0:T(4,128)} %prior.1) | copy-start | bytes 6148
  2.7 1.0 %copy-start.10 = (f32[8]{0:T(128)S(1)}, f32[8]{0:T(128)}, u32[]{:S(2)}) copy-start(f32[8]{0:T(128)} %attenuation.1) | copy-start | bytes 100
  2.7 1.0 %copy-start.11 = (f32[8]{0:T(128)S(1)}, f32[8]{0:T(128)}, u32[]{:S(2)}) copy-start(f32[8]{0:T(128)} %drain.1) | copy-start | bytes 100
  2.7 1.0 %copy-start.12 = (f32[8]{0:T(128)S(1)}, f32[8]{0:T(128)}, u32[]{:S(2)}) copy-start(f32[8]{0:T(128)} %diffusivity.1) | copy-start | bytes 100

commit v2 on v1

--- a/solution.py
+++ b/solution.py
@@ -14,8 +14,11 @@
 OWN = 128
 ROWS = 4
 COLS = 128
-CHUNKS = 4
+CHUNKS = 8
 WIDTH = COLS // CHUNKS
+ORDER = (1, 0, 2, 3, 4, 5, 6, 7)
+PARTS = 4
+PART = COLS // PARTS
 PAD = 16
 F32 = jnp.float32
 BF16 = jnp.bfloat16
@@ -57,14 +60,14 @@
 
 
 def kernel(
-    src, label, prior, attenuation, drain, diffusivity,
+    wave, lens, label, prior, attenuation, drain, diffusivity,
     fine_c, fine_s, coarse_c, coarse_s, far_c, far_s, near_c, near_s,
     field, later,
-    S, VA, VB, M, R, Y, W,
+    raw, S, VA, VB, M, R, Y, W,
     synth_c, synth_s, anal_c, anal_s,
     factors_fine, factors_coarse, factors_far, factors_near,
     early, late, heat_rows, heat_out, wide,
-    load_sem, row_send, row_recv, col_send, col_recv, corner_send, corner_recv,
+    raw_sem, load_sem, row_send, row_recv, col_send, col_recv, corner_send, corner_recv,
     early_send, early_recv, late_send, late_recv,
     one_send, one_recv, two_send, two_recv, heat_send, heat_recv,
 ):
@@ -96,6 +99,12 @@
             ok = one if ok is None else jnp.logical_and(ok, one)
         return ok
 
+    raws = []
+    for p in range(2):
+        for row in range(ROWS):
+            copy = pltpu.make_async_copy(wave.at[p, :, row, :], raw.at[p, row], raw_sem.at[p, row])
+            copy.start()
+            raws.append((p, row, copy))
     loads = []
     for i, (a, b) in enumerate((
         (fine_c, factors_fine.at[0]), (fine_s, factors_fine.at[1]),
@@ -142,6 +151,11 @@
             pl.semaphore_signal(barrier, inc=1, device_id=(harm, tx + dy, ty + dx), device_id_type=pl.DeviceIdType.MESH)
     for j in range(4):
         pl.semaphore_signal(barrier, inc=1, device_id=(j, tx, far_ty), device_id_type=pl.DeviceIdType.MESH)
+
+    weight = 0.25 + 0.75 * lens[...].astype(F32)
+    for p, row, copy in raws:
+        copy.wait()
+        S[p, 4 + row, PAD:PAD + COLS, :] = jnp.transpose(raw[p, row] * weight[row:row + 1, :])
 
     kinds = label[...]
     conduct = jnp.zeros((ROWS, COLS), F32)
@@ -163,14 +177,14 @@
 
     def row_copy(side, c):
         return remote(
-            src.at[:, :, pl.ds(c * WIDTH, WIDTH), :],
+            S.at[:, 4:8, pl.ds(PAD + c * WIDTH, WIDTH), :],
             S.at[:, pl.ds(8 * side, 4), pl.ds(PAD + c * WIDTH, WIDTH), :],
             row_send.at[side, c], row_recv.at[side, c], (harm, tx + 1 - 2 * side, ty),
         )
 
     def col_copy(side):
         return remote(
-            src.at[:, :, pl.ds(0 if side else COLS - 8, 8), :],
+            S.at[:, 4:8, pl.ds(PAD if side else PAD + COLS - 8, 8), :],
             S.at[:, 4:8, pl.ds(PAD + COLS if side else PAD - 8, 8), :],
             col_send.at[side], col_recv.at[side], (harm, tx, ty + 1 - 2 * side),
         )
@@ -200,12 +214,15 @@
         @pl.when(to_col(side))
         def _():
             col_copy(side).start()
-    for c in range(CHUNKS):
+    def start_rows(c):
         for side in (0, 1):
             @pl.when(to_side(side))
             def _():
                 row_copy(side, c).start()
 
+    for c in range(3):
+        start_rows(c)
+
     def early_copy(dy, dx):
         slot = 3 * (dy + 1) + dx + 1
         return remote(
@@ -224,10 +241,6 @@
         @pl.when(inside(dy, dx))
         def _():
             early_copy(dy, dx).start()
-
-    for p in range(2):
-        for row in range(ROWS):
-            S[p, 4 + row, PAD:PAD + COLS, :] = src[p, row]
 
     lane = lax.broadcasted_iota(jnp.int32, (1, OWN), 1)
     gain = diffraction_gain / (harm * OWN + lane + 1).astype(F32)
@@ -285,15 +298,15 @@
 
     def two_copy(c, j):
         return remote(
-            Y.at[j, :, pl.ds(c * WIDTH, WIDTH), :],
-            field.at[own_row, :, pl.ds(c * WIDTH, WIDTH), :],
+            Y.at[j, :, pl.ds(c * PART, PART), :],
+            field.at[own_row, :, pl.ds(c * PART, PART), :],
             two_send.at[c, j], two_recv.at[c, own_row], (j, tx, far_ty),
         )
 
     def two_arrival(c, row):
         return remote(
-            Y.at[0, :, pl.ds(c * WIDTH, WIDTH), :],
-            field.at[row, :, pl.ds(c * WIDTH, WIDTH), :],
+            Y.at[0, :, pl.ds(c * PART, PART), :],
+            field.at[row, :, pl.ds(c * PART, PART), :],
             two_send.at[c, 0], two_recv.at[c, row], owner(row),
         )
 
@@ -354,13 +367,19 @@
         lax.fori_loop(0, HALF // 16, by_harmonic, 0)
 
     forward(0)
+    for c in range(3, 6):
+        start_rows(c)
     forward(1)
-    wait_rows(0)
-    wait_corners(0)
-    for c in range(CHUNKS):
-        if c + 1 < CHUNKS:
-            wait_rows(c + 1)
-        else:
+    for c in range(6, CHUNKS):
+        start_rows(c)
+    arrived = 0
+    for c in ORDER:
+        while arrived < min(c + 2, CHUNKS):
+            wait_rows(arrived)
+            arrived += 1
+        if c == 0:
+            wait_corners(0)
+        if c == CHUNKS - 1:
             wait_corners(1)
         stencil(c)
         for row in range(ROWS):
@@ -373,9 +392,10 @@
     imag_factor = numbers * (nonlinear_gain / HARMONICS * 2.0 * scale)
 
     def nonlinear(c, carry):
-        for j in range(4):
-            one_arrival(c, j).wait_recv()
-        cols = pl.ds(pl.multiple_of(c * WIDTH, WIDTH), WIDTH)
+        for k in range(PART // WIDTH):
+            for j in range(4):
+                one_arrival(c * (PART // WIDTH) + k, j).wait_recv()
+        cols = pl.ds(pl.multiple_of(c * PART, PART), PART)
         real = jnp.concatenate([R[j, 0, cols, :] for j in range(4)], axis=1)
         imag = jnp.concatenate([R[j, 1, cols, :] for j in range(4)], axis=1)
         even = product(real, synth_c[0], synth_c[1])
@@ -389,11 +409,15 @@
         for j in range(4):
             Y[j, 0, cols, :] = real[:, 128 * j:128 * (j + 1)]
             Y[j, 1, cols, :] = imag[:, 128 * j:128 * (j + 1)]
-        for j in range(4):
-            two_copy(c, j).start()
+
+        @pl.when(c < PARTS - 1)
+        def _():
+            for j in range(4):
+                two_copy(c, j).start()
+
         return carry
 
-    lax.fori_loop(0, CHUNKS, nonlinear, 0)
+    lax.fori_loop(0, PARTS, nonlinear, 0)
 
     heat_out[...] = lax.dot_general(
         jnp.ones((8, OWN), F32), W[...], (((1,), (1,)), ((), ())),
@@ -405,6 +429,8 @@
 
     for j in range(4):
         heat_copy(j).start()
+    for j in range(4):
+        two_copy(PARTS - 1, j).start()
     for row in range(ROWS):
         remote(heat_out, heat_rows.at[row], heat_send.at[0], heat_recv.at[row], owner(row)).wait_recv()
     for row in range(ROWS):
@@ -469,6 +495,8 @@
     for c in range(CHUNKS):
         for j in range(4):
             one_copy(c, j).wait_send()
+    for c in range(PARTS):
+        for j in range(4):
             two_copy(c, j).wait_send()
             two_arrival(c, j).wait_recv()
 
@@ -477,11 +505,10 @@
     factors = table_factors()
 
     def body(wave, lens, label, prior, attenuation, drain, diffusivity):
-        weight = 0.25 + 0.75 * lens.astype(F32)
-        src = jnp.transpose(wave * weight, (0, 2, 3, 1))
         vmem = pl.BlockSpec(memory_space=pltpu.VMEM)
         smem = pl.BlockSpec(memory_space=pltpu.SMEM)
-        hbm = pl.BlockSpec(memory_space=pl.ANY)
+        hbm = pl.BlockSpec(memory_space=pltpu.HBM)
+        anywhere = pl.BlockSpec(memory_space=pl.ANY)
         dma = pltpu.SemaphoreType.DMA
         field, later = pl.pallas_call(
             kernel,
@@ -489,9 +516,10 @@
                 jax.ShapeDtypeStruct((ROWS, 2, COLS, OWN), F32),
                 jax.ShapeDtypeStruct((ROWS, COLS), F32),
             ),
-            in_specs=[vmem, vmem, vmem, smem, smem, smem] + [hbm] * 8,
-            out_specs=(hbm, vmem),
+            in_specs=[hbm, vmem, vmem, vmem, smem, smem, smem] + [hbm] * 8,
+            out_specs=(anywhere, vmem),
             scratch_shapes=[
+                pltpu.VMEM((2, ROWS, OWN, COLS), F32),
                 pltpu.VMEM((2, 12, COLS + 2 * PAD, OWN), F32),
                 pltpu.VMEM((2, 12, WIDTH + 2 * PAD, OWN), F32),
                 pltpu.VMEM((2, 12, WIDTH + 2 * PAD, OWN), F32),
@@ -512,15 +540,15 @@
                 pltpu.VMEM((ROWS, 1, COLS), F32),
                 pltpu.VMEM((1, COLS), F32),
                 pltpu.VMEM((4, 16, 3 * COLS), F32),
-                dma((8,)), dma((2, CHUNKS)), dma((2, CHUNKS)), dma((2,)), dma((2,)), dma((2, 2)), dma((2, 2)),
+                dma((2, ROWS)), dma((8,)), dma((2, CHUNKS)), dma((2, CHUNKS)), dma((2,)), dma((2,)), dma((2, 2)), dma((2, 2)),
                 dma((9,)), dma((9,)), dma((9,)), dma((9,)),
-                dma((CHUNKS, 4)), dma((CHUNKS, 4)), dma((CHUNKS, 4)), dma((CHUNKS, 4)), dma((4,)), dma((4,)),
+                dma((CHUNKS, 4)), dma((CHUNKS, 4)), dma((PARTS, 4)), dma((PARTS, 4)), dma((4,)), dma((4,)),
             ],
             compiler_params=pltpu.CompilerParams(
-                collective_id=0, has_side_effects=True, vmem_limit_bytes=48 << 20
+                collective_id=0, has_side_effects=True
             ),
             name="march",
-        )(src, label, prior, attenuation, drain, diffusivity, *[jnp.asarray(f) for f in factors])
+        )(wave, lens, label, prior, attenuation, drain, diffusivity, *[jnp.asarray(f) for f in factors])
         return jnp.transpose(field, (1, 3, 0, 2)), later
 
     in_specs = (P(None, "harm", "tx", "ty"), P("tx", "ty"), P("tx", "ty"), P("tx", "ty"), P(), P(), P())

time: 90 us -> 78.8 us (0.88); the launches traced: 88.9 us -> 78.6 us
  Pallas kernels: 83.6 us -> 75.4 us
  local copies, waits for them, and re-layouts: 3.69 us -> 2.62 us
    pallas_call x1, Pallas kernels: 83.6 us -> 75.4 us  [body(): pl.pallas_call(kernel, out_shape=(jax.ShapeDtypeStruct((ROWS, 2, COLS, OW...]
    unnamed x29 -> x4, local copies, waits for them, and re-layouts: 3.69 us -> 2.62 us
where the time goes in v2:
time: 78.8 us; the launch traced here: 78.6 us
  Pallas kernels  75.4 us (96%)
  local copies, waits for them, and re-layouts  2.62 us (3%)
    pallas_call x1, Pallas kernels, body(): pl.pallas_call(kernel, out_shape=(jax.ShapeDtypeStruct((ROWS, 2, COLS, OW...  75.4 us
    unnamed x4, local copies, waits for them, and re-layouts  2.62 us

profile of v2, /device:TPU:6, one launch (start us, length us, event | category | flops | bytes accessed | tf_op | source)
XLA Modules:
  0.0 78.6 jit_solution(312991047171112297)
XLA Ops:
  0.6 75.4 %march.1 = (f32[4,2,128,128]{3,2,1,0:T(8,128)}, f32[4,128]{1,0:T(4,128)}) custom-call(f32[2,128,4,128]{3,2,1,0:T(4,128)} %wave.1, s32[4,128]{1,0:T(4,128)} %lens.1, s32[4,128]{1,0:T(4,128)} %label.1, f32[4,128]{1,0:T(4,128)} %prior.1, f32[8]{0:T(128)} %attenuation.1, f32[8]{0:T(128)} %drain.1, f32[8]{0:T(128)} %diffusivity.1, ...), custom_call_target="tpu_custom_call" | custom-call | tf_op jit(solution)/shard_map/march/pallas_call | solution.py:513
  76.0 0.0 copy-start
  76.0 2.0 %copy.17 = f32[2,128,4,128]{3,2,1,0:T(4,128)} copy(f32[2,128,4,128]{1,3,0,2:T(8,128)} %bitcast.1) | data formatting | bytes 1048576
  78.1 0.0 copy-done
  78.1 0.6 copy.19
Async XLA Ops:
  76.0 2.0 %copy-start = (f32[4,128]{1,0:T(4,128)S(1)}, f32[4,128]{1,0:T(4,128)}, u32[]{:S(2)}) copy-start(f32[4,128]{1,0:T(4,128)} %get-tuple-element.11) | copy-start | bytes 6148

commit v3 on v2

--- a/solution.py
+++ b/solution.py
@@ -14,9 +14,11 @@
 OWN = 128
 ROWS = 4
 COLS = 128
-CHUNKS = 8
-WIDTH = COLS // CHUNKS
-ORDER = (1, 0, 2, 3, 4, 5, 6, 7)
+SEGMENTS = [(8 * i, 8) for i in range(4)] + [(16 * i, 16) for i in range(2, 8)]
+ORDER = (1, 2, 0, 3, 4, 5, 6, 7, 8, 9)
+CHUNKS = len(SEGMENTS)
+WIDEST = 16
+EARLY_PARTS = 2
 PARTS = 4
 PART = COLS // PARTS
 PAD = 16
@@ -60,14 +62,14 @@
 
 
 def kernel(
-    wave, lens, label, prior, attenuation, drain, diffusivity,
+    wave, lens_in, label_in, prior_in, attenuation, drain, diffusivity,
     fine_c, fine_s, coarse_c, coarse_s, far_c, far_s, near_c, near_s,
     field, later,
-    raw, S, VA, VB, M, R, Y, W,
+    lens, label, prior, later_rows, raw, S, VA, VB, M, R, Y, W,
     synth_c, synth_s, anal_c, anal_s,
     factors_fine, factors_coarse, factors_far, factors_near,
     early, late, heat_rows, heat_out, wide,
-    raw_sem, load_sem, row_send, row_recv, col_send, col_recv, corner_send, corner_recv,
+    small_sem, raw_sem, load_sem, row_send, row_recv, col_send, col_recv, corner_send, corner_recv,
     early_send, early_recv, late_send, late_recv,
     one_send, one_recv, two_send, two_recv, heat_send, heat_recv,
 ):
@@ -99,6 +101,50 @@
             ok = one if ok is None else jnp.logical_and(ok, one)
         return ok
 
+    @pl.when(tx == 0)
+    def _():
+        S[:, 0:4] = jnp.zeros((2, 4, COLS + 2 * PAD, OWN), F32)
+        for dx in range(3):
+            early[0, dx] = jnp.zeros((4, ROWS, COLS), F32)
+            late[0, dx] = jnp.zeros((ROWS, COLS), F32)
+
+    @pl.when(tx == TX - 1)
+    def _():
+        S[:, 8:12] = jnp.zeros((2, 4, COLS + 2 * PAD, OWN), F32)
+        for dx in range(3):
+            early[2, dx] = jnp.zeros((4, ROWS, COLS), F32)
+            late[2, dx] = jnp.zeros((ROWS, COLS), F32)
+
+    @pl.when(ty == 0)
+    def _():
+        S[:, :, 8:16] = jnp.zeros((2, 12, 8, OWN), F32)
+        for dy in range(3):
+            early[dy, 0] = jnp.zeros((4, ROWS, COLS), F32)
+
+    @pl.when(ty == TY - 1)
+    def _():
+        S[:, :, PAD + COLS:PAD + COLS + 8] = jnp.zeros((2, 12, 8, OWN), F32)
+        for dy in range(3):
+            early[dy, 2] = jnp.zeros((4, ROWS, COLS), F32)
+
+    barrier = pltpu.get_barrier_semaphore()
+    for dy, dx in AROUND:
+        @pl.when(inside(dy, dx))
+        def _():
+            pl.semaphore_signal(barrier, inc=1, device_id=(harm, tx + dy, ty + dx), device_id_type=pl.DeviceIdType.MESH)
+    for dx in (-1, 0, 1):
+        for j in range(4):
+            pl.semaphore_signal(
+                barrier, inc=1, device_id=(j, tx, (ty + dx + 4) % TY), device_id_type=pl.DeviceIdType.MESH
+            )
+
+    smalls = []
+    for i, (a, b) in enumerate((
+        (lens_in, lens), (label_in, label), (prior_in, prior),
+    )):
+        copy = pltpu.make_async_copy(a, b, small_sem.at[i])
+        copy.start()
+        smalls.append(copy)
     raws = []
     for p in range(2):
         for row in range(ROWS):
@@ -116,42 +162,8 @@
         copy.start()
         loads.append(copy)
 
-    @pl.when(tx == 0)
-    def _():
-        S[:, 0:4] = jnp.zeros((2, 4, COLS + 2 * PAD, OWN), F32)
-        for dx in range(3):
-            early[0, dx] = jnp.zeros((3, ROWS, COLS), F32)
-            late[0, dx] = jnp.zeros((ROWS, COLS), F32)
-
-    @pl.when(tx == TX - 1)
-    def _():
-        S[:, 8:12] = jnp.zeros((2, 4, COLS + 2 * PAD, OWN), F32)
-        for dx in range(3):
-            early[2, dx] = jnp.zeros((3, ROWS, COLS), F32)
-            late[2, dx] = jnp.zeros((ROWS, COLS), F32)
-
-    @pl.when(ty == 0)
-    def _():
-        S[:, :, 8:16] = jnp.zeros((2, 12, 8, OWN), F32)
-        for dy in range(3):
-            early[dy, 0] = jnp.zeros((3, ROWS, COLS), F32)
-            late[dy, 0] = jnp.zeros((ROWS, COLS), F32)
-
-    @pl.when(ty == TY - 1)
-    def _():
-        S[:, :, PAD + COLS:PAD + COLS + 8] = jnp.zeros((2, 12, 8, OWN), F32)
-        for dy in range(3):
-            early[dy, 2] = jnp.zeros((3, ROWS, COLS), F32)
-            late[dy, 2] = jnp.zeros((ROWS, COLS), F32)
-
-    barrier = pltpu.get_barrier_semaphore()
-    for dy, dx in AROUND:
-        @pl.when(inside(dy, dx))
-        def _():
-            pl.semaphore_signal(barrier, inc=1, device_id=(harm, tx + dy, ty + dx), device_id_type=pl.DeviceIdType.MESH)
-    for j in range(4):
-        pl.semaphore_signal(barrier, inc=1, device_id=(j, tx, far_ty), device_id_type=pl.DeviceIdType.MESH)
-
+    for copy in smalls:
+        copy.wait()
     weight = 0.25 + 0.75 * lens[...].astype(F32)
     for p, row, copy in raws:
         copy.wait()
@@ -169,16 +181,17 @@
     early[1, 1, 0] = prior[...]
     early[1, 1, 1] = conduct
     early[1, 1, 2] = perfuse
+    early[1, 1, 3] = absorb
 
     def edges(at, count):
         return jnp.where(at == 0, 1, 0) + jnp.where(at == count - 1, 1, 0)
 
-    pl.semaphore_wait(barrier, (3 - edges(tx, TX)) * (3 - edges(ty, TY)) + 3)
+    pl.semaphore_wait(barrier, (3 - edges(tx, TX)) * (3 - edges(ty, TY)) + 11)
 
     def row_copy(side, c):
         return remote(
-            S.at[:, 4:8, pl.ds(PAD + c * WIDTH, WIDTH), :],
-            S.at[:, pl.ds(8 * side, 4), pl.ds(PAD + c * WIDTH, WIDTH), :],
+            S.at[:, 4:8, pl.ds(PAD + SEGMENTS[c][0], SEGMENTS[c][1]), :],
+            S.at[:, pl.ds(8 * side, 4), pl.ds(PAD + SEGMENTS[c][0], SEGMENTS[c][1]), :],
             row_send.at[side, c], row_recv.at[side, c], (harm, tx + 1 - 2 * side, ty),
         )
 
@@ -220,7 +233,7 @@
             def _():
                 row_copy(side, c).start()
 
-    for c in range(3):
+    for c in range(4):
         start_rows(c)
 
     def early_copy(dy, dx):
@@ -230,11 +243,14 @@
             (harm, tx + dy, ty + dx),
         )
 
-    def late_copy(dy, dx):
-        slot = 3 * (dy + 1) + dx + 1
-        return remote(
-            late.at[1, 1], late.at[1 - dy, 1 - dx], late_send.at[slot], late_recv.at[8 - slot],
-            (harm, tx + dy, ty + dx),
+    def late_copy(dy):
+        return remote(
+            late.at[1], late.at[1 - dy], late_send.at[1 + dy], late_recv.at[1 - dy], (harm, tx + dy, ty),
+        )
+
+    def late_arrival(dy):
+        return remote(
+            late.at[1], late.at[1 + dy], late_send.at[1 + dy], late_recv.at[1 + dy], (harm, tx + dy, ty),
         )
 
     for dy, dx in AROUND:
@@ -250,11 +266,11 @@
         return jnp.where(jnp.logical_and(at >= 0, at < TX * ROWS), 1.0, 0.0).astype(F32)
 
     def stencil(c):
-        base = c * WIDTH
+        base, width = SEGMENTS[c]
         for k, source, target in ((1, S, VA), (2, VA, VB), (3, VB, VA), (4, VA, M)):
-            low, count = (PAD, WIDTH) if k == 4 else (8, WIDTH + 16)
-            shift = base if k == 1 else 0
-            at = ty * COLS + base + low - PAD + lax.broadcasted_iota(jnp.int32, (count, OWN), 0)
+            low, count = (12, width) if k == 4 else (8, width + 8)
+            shift = base + 4 if k == 1 else 0
+            at = ty * COLS + base + low + 4 - PAD + lax.broadcasted_iota(jnp.int32, (count, OWN), 0)
             valid = jnp.logical_and(at >= 0, at < TY * COLS)
             g = jnp.where(valid, gain * (1.0 / (5 - k)), 0.0)
 
@@ -270,8 +286,8 @@
                         + source[p, row, pl.ds(shift + low - 1, count), :]
                         - 4.0 * center
                     )
-                real = S[0, row, pl.ds(base + low, count), :] - gr * laps[1]
-                imag = S[1, row, pl.ds(base + low, count), :] + gr * laps[0]
+                real = S[0, row, pl.ds(base + 4 + low, count), :] - gr * laps[1]
+                imag = S[1, row, pl.ds(base + 4 + low, count), :] + gr * laps[0]
                 if k == 4:
                     target[0, row - 4, pl.ds(base, count), :] = real
                     target[1, row - 4, pl.ds(base, count), :] = imag
@@ -284,15 +300,15 @@
 
     def one_copy(c, row):
         return remote(
-            M.at[:, row, pl.ds(c * WIDTH, WIDTH), :],
-            R.at[harm, :, pl.ds(c * WIDTH, WIDTH), :],
+            M.at[:, row, pl.ds(*SEGMENTS[c]), :],
+            R.at[harm, :, pl.ds(*SEGMENTS[c]), :],
             one_send.at[c, row], one_recv.at[c, harm], owner(row),
         )
 
-    def one_arrival(c, j):
-        return remote(
-            M.at[:, 0, pl.ds(c * WIDTH, WIDTH), :],
-            R.at[j, :, pl.ds(c * WIDTH, WIDTH), :],
+    def one_arrival(c, at, width, j):
+        return remote(
+            M.at[:, 0, pl.ds(at, width), :],
+            R.at[j, :, pl.ds(at, width), :],
             one_send.at[c, 0], one_recv.at[c, j], (j, tx, far_ty),
         )
 
@@ -367,10 +383,10 @@
         lax.fori_loop(0, HALF // 16, by_harmonic, 0)
 
     forward(0)
-    for c in range(3, 6):
+    for c in range(4, 7):
         start_rows(c)
     forward(1)
-    for c in range(6, CHUNKS):
+    for c in range(7, CHUNKS):
         start_rows(c)
     arrived = 0
     for c in ORDER:
@@ -392,9 +408,18 @@
     imag_factor = numbers * (nonlinear_gain / HARMONICS * 2.0 * scale)
 
     def nonlinear(c, carry):
-        for k in range(PART // WIDTH):
-            for j in range(4):
-                one_arrival(c * (PART // WIDTH) + k, j).wait_recv()
+        @pl.when(c == 0)
+        def _():
+            for k in range(4):
+                for j in range(4):
+                    one_arrival(k, 8 * k, 8, j).wait_recv()
+
+        @pl.when(c > 0)
+        def _():
+            for k in range(2):
+                for j in range(4):
+                    one_arrival(2 + 2 * c + k, pl.multiple_of(c * PART + 16 * k, 16), 16, j).wait_recv()
+
         cols = pl.ds(pl.multiple_of(c * PART, PART), PART)
         real = jnp.concatenate([R[j, 0, cols, :] for j in range(4)], axis=1)
         imag = jnp.concatenate([R[j, 1, cols, :] for j in range(4)], axis=1)
@@ -410,7 +435,7 @@
             Y[j, 0, cols, :] = real[:, 128 * j:128 * (j + 1)]
             Y[j, 1, cols, :] = imag[:, 128 * j:128 * (j + 1)]
 
-        @pl.when(c < PARTS - 1)
+        @pl.when(c < EARLY_PARTS)
         def _():
             for j in range(4):
                 two_copy(c, j).start()
@@ -424,42 +449,55 @@
         precision=lax.Precision.HIGHEST, preferred_element_type=F32,
     )[0:1]
 
-    def heat_copy(j):
-        return remote(heat_out, heat_rows.at[own_row], heat_send.at[j], heat_recv.at[own_row], (j, tx, far_ty))
-
-    for j in range(4):
-        heat_copy(j).start()
-    for j in range(4):
-        two_copy(PARTS - 1, j).start()
-    for row in range(ROWS):
-        remote(heat_out, heat_rows.at[row], heat_send.at[0], heat_recv.at[row], owner(row)).wait_recv()
-    for row in range(ROWS):
-        late[1, 1, row:row + 1, :] = absorb[row:row + 1] * heat_rows[row] / float(HARMONICS * HARMONICS)
+    def heat_copy(dx, j):
+        return remote(
+            heat_out, heat_rows.at[1 - dx, own_row], heat_send.at[1 + dx, j], heat_recv.at[1 - dx, own_row],
+            (j, tx, (ty + dx + 4) % TY),
+        )
+
+    def heat_arrival(dx, row):
+        return remote(
+            heat_out, heat_rows.at[1 + dx, row], heat_send.at[1, 0], heat_recv.at[1 + dx, row],
+            (row, tx, far_ty),
+        )
+
+    for dx in (-1, 0, 1):
+        for j in range(4):
+            heat_copy(dx, j).start()
+    for c in range(EARLY_PARTS, PARTS):
+        for j in range(4):
+            two_copy(c, j).start()
+    for dx in (-1, 0, 1):
+        for row in range(ROWS):
+            heat_arrival(dx, row).wait_recv()
+    for dx in range(3):
+        for row in range(ROWS):
+            late[1, dx, row:row + 1, :] = heat_rows[dx, row]
+    for dy in (-1, 1):
+        @pl.when(inside(dy, 0))
+        def _():
+            late_copy(dy).start()
     for dy, dx in AROUND:
         @pl.when(inside(dy, dx))
         def _():
-            late_copy(dy, dx).start()
-    for dy, dx in AROUND:
-        @pl.when(inside(dy, dx))
-        def _():
             early_copy(-dy, -dx).wait_recv()
-    for dy, dx in AROUND:
-        @pl.when(inside(dy, dx))
-        def _():
-            late_copy(-dy, -dx).wait_recv()
+    for dy in (-1, 1):
+        @pl.when(inside(dy, 0))
+        def _():
+            late_arrival(dy).wait_recv()
     for dy in range(3):
         for dx in range(3):
             rows = slice(4 * dy, 4 * dy + 4)
             cols = slice(128 * dx, 128 * dx + 128)
-            for k in range(3):
+            for k in range(4):
                 wide[k, rows, cols] = early[dy, dx, k]
-            wide[3, rows, cols] = late[dy, dx]
-    for k in range(4):
+            wide[4, rows, cols] = late[dy, dx]
+    for k in range(5):
         wide[k, 12:16, :] = jnp.zeros((4, 3 * COLS), F32)
     temperature = wide[0]
     wide_conduct = wide[1]
     wide_perfuse = wide[2]
-    wide_deposit = wide[3]
+    wide_deposit = wide[3] * wide[4] / float(HARMONICS * HARMONICS)
     for _ in range(4):
         lap = (
             pltpu.roll(temperature, 15, 0) + pltpu.roll(temperature, 1, 0)
@@ -468,7 +506,9 @@
         )
         temperature = temperature + wide_conduct * lap - wide_perfuse * temperature + wide_deposit
     wide[0] = temperature
-    later[...] = wide[0, 4:8, COLS:2 * COLS]
+    later_rows[...] = wide[0, 4:8, COLS:2 * COLS]
+    result = pltpu.make_async_copy(later_rows, later, small_sem.at[3])
+    result.start()
 
     for side in (0, 1):
         @pl.when(to_col(side))
@@ -489,9 +529,14 @@
         @pl.when(inside(dy, dx))
         def _():
             early_copy(dy, dx).wait_send()
-            late_copy(dy, dx).wait_send()
-    for j in range(4):
-        heat_copy(j).wait_send()
+    for dy in (-1, 1):
+        @pl.when(inside(dy, 0))
+        def _():
+            late_copy(dy).wait_send()
+    for dx in (-1, 0, 1):
+        for j in range(4):
+            heat_copy(dx, j).wait_send()
+    result.wait()
     for c in range(CHUNKS):
         for j in range(4):
             one_copy(c, j).wait_send()
@@ -505,10 +550,8 @@
     factors = table_factors()
 
     def body(wave, lens, label, prior, attenuation, drain, diffusivity):
-        vmem = pl.BlockSpec(memory_space=pltpu.VMEM)
         smem = pl.BlockSpec(memory_space=pltpu.SMEM)
         hbm = pl.BlockSpec(memory_space=pltpu.HBM)
-        anywhere = pl.BlockSpec(memory_space=pl.ANY)
         dma = pltpu.SemaphoreType.DMA
         field, later = pl.pallas_call(
             kernel,
@@ -516,13 +559,15 @@
                 jax.ShapeDtypeStruct((ROWS, 2, COLS, OWN), F32),
                 jax.ShapeDtypeStruct((ROWS, COLS), F32),
             ),
-            in_specs=[hbm, vmem, vmem, vmem, smem, smem, smem] + [hbm] * 8,
-            out_specs=(anywhere, vmem),
+            in_specs=[hbm] * 4 + [smem] * 3 + [hbm] * 8,
+            out_specs=(hbm, hbm),
             scratch_shapes=[
+                pltpu.VMEM((ROWS, COLS), jnp.int32), pltpu.VMEM((ROWS, COLS), jnp.int32), pltpu.VMEM((ROWS, COLS), F32),
+                pltpu.VMEM((ROWS, COLS), F32),
                 pltpu.VMEM((2, ROWS, OWN, COLS), F32),
                 pltpu.VMEM((2, 12, COLS + 2 * PAD, OWN), F32),
-                pltpu.VMEM((2, 12, WIDTH + 2 * PAD, OWN), F32),
-                pltpu.VMEM((2, 12, WIDTH + 2 * PAD, OWN), F32),
+                pltpu.VMEM((2, 12, WIDEST + 2 * PAD, OWN), F32),
+                pltpu.VMEM((2, 12, WIDEST + 2 * PAD, OWN), F32),
                 pltpu.VMEM((2, ROWS, COLS, OWN), F32),
                 pltpu.VMEM((4, 2, COLS, OWN), F32),
                 pltpu.VMEM((4, 2, COLS, OWN), F32),
@@ -535,14 +580,14 @@
                 pltpu.VMEM((2, 8, 16, 128), F32),
                 pltpu.VMEM((2, 64, HARMONICS), F32),
                 pltpu.VMEM((2, 16, HARMONICS), F32),
-                pltpu.VMEM((3, 3, 3, ROWS, COLS), F32),
+                pltpu.VMEM((3, 3, 4, ROWS, COLS), F32),
                 pltpu.VMEM((3, 3, ROWS, COLS), F32),
-                pltpu.VMEM((ROWS, 1, COLS), F32),
+                pltpu.VMEM((3, ROWS, 1, COLS), F32),
                 pltpu.VMEM((1, COLS), F32),
-                pltpu.VMEM((4, 16, 3 * COLS), F32),
-                dma((2, ROWS)), dma((8,)), dma((2, CHUNKS)), dma((2, CHUNKS)), dma((2,)), dma((2,)), dma((2, 2)), dma((2, 2)),
-                dma((9,)), dma((9,)), dma((9,)), dma((9,)),
-                dma((CHUNKS, 4)), dma((CHUNKS, 4)), dma((PARTS, 4)), dma((PARTS, 4)), dma((4,)), dma((4,)),
+                pltpu.VMEM((5, 16, 3 * COLS), F32),
+                dma((4,)), dma((2, ROWS)), dma((8,)), dma((2, CHUNKS)), dma((2, CHUNKS)), dma((2,)), dma((2,)), dma((2, 2)), dma((2, 2)),
+                dma((9,)), dma((9,)), dma((3,)), dma((3,)),
+                dma((CHUNKS, 4)), dma((CHUNKS, 4)), dma((PARTS, 4)), dma((PARTS, 4)), dma((3, 4)), dma((3, 4)),
             ],
             compiler_params=pltpu.CompilerParams(
                 collective_id=0, has_side_effects=True

time: 78.8 us -> 74.2 us (0.942)
  Pallas kernels: 75.4 us -> 70.8 us
    pallas_call x1, Pallas kernels: 75.4 us -> 70.8 us  [body(): pl.pallas_call(kernel, out_shape=(jax.ShapeDtypeStruct((ROWS, 2, COLS, OW...]
where the time goes in v3:
time: 74.2 us; the launch traced here: 74 us
  Pallas kernels  70.8 us (95%)
  local copies, waits for them, and re-layouts  2.62 us (4%)
    pallas_call x1, Pallas kernels, body(): pl.pallas_call(kernel, out_shape=(jax.ShapeDtypeStruct((ROWS, 2, COLS, OW...  70.8 us
    unnamed x4, local copies, waits for them, and re-layouts  2.62 us

profile of v3, /device:TPU:6, one launch (start us, length us, event | category | flops | bytes accessed | tf_op | source)
XLA Modules:
  0.0 74.0 jit_solution(7700426508469806769)
XLA Ops:
  0.6 70.8 %march.1 = (f32[4,2,128,128]{3,2,1,0:T(8,128)}, f32[4,128]{1,0:T(4,128)}) custom-call(f32[2,128,4,128]{3,2,1,0:T(4,128)} %wave.1, s32[4,128]{1,0:T(4,128)} %lens_in.1, s32[4,128]{1,0:T(4,128)} %label_in.1, f32[4,128]{1,0:T(4,128)} %prior_in.1, f32[8]{0:T(128)} %attenuation.1, f32[8]{0:T(128)} %drain.1, f32[8]{0:T(128)} %diffusivity.1, ...), custom_call_target="tpu_custom_call" | custom-call | tf_op jit(solution)/shard_map/march/pallas_call | solution.py:556
  71.4 0.0 copy-start
  71.4 2.0 %copy.17 = f32[2,128,4,128]{3,2,1,0:T(4,128)} copy(f32[2,128,4,128]{1,3,0,2:T(8,128)} %bitcast.1) | data formatting | bytes 1048576
  73.5 0.0 copy-done
  73.5 0.6 copy.19
Async XLA Ops:
  71.4 2.0 %copy-start = (f32[4,128]{1,0:T(4,128)S(1)}, f32[4,128]{1,0:T(4,128)}, u32[]{:S(2)}) copy-start(f32[4,128]{1,0:T(4,128)} %get-tuple-element.11) | copy-start | bytes 6148

commit v4 on v3

--- a/solution.py
+++ b/solution.py
@@ -62,10 +62,10 @@
 
 
 def kernel(
-    wave, lens_in, label_in, prior_in, attenuation, drain, diffusivity,
+    wave, lens_in, label_in, prior_in, attenuation_in, drain_in, diffusivity_in,
     fine_c, fine_s, coarse_c, coarse_s, far_c, far_s, near_c, near_s,
     field, later,
-    lens, label, prior, later_rows, raw, S, VA, VB, M, R, Y, W,
+    lens, label, prior, attenuation, drain, diffusivity, raw, S, VA, VB, M, R, Y, W,
     synth_c, synth_s, anal_c, anal_s,
     factors_fine, factors_coarse, factors_far, factors_near,
     early, late, heat_rows, heat_out, wide,
@@ -141,6 +141,7 @@
     smalls = []
     for i, (a, b) in enumerate((
         (lens_in, lens), (label_in, label), (prior_in, prior),
+        (attenuation_in, attenuation), (drain_in, drain), (diffusivity_in, diffusivity),
     )):
         copy = pltpu.make_async_copy(a, b, small_sem.at[i])
         copy.start()
@@ -506,9 +507,7 @@
         )
         temperature = temperature + wide_conduct * lap - wide_perfuse * temperature + wide_deposit
     wide[0] = temperature
-    later_rows[...] = wide[0, 4:8, COLS:2 * COLS]
-    result = pltpu.make_async_copy(later_rows, later, small_sem.at[3])
-    result.start()
+    later[...] = wide[0, 4:8, COLS:2 * COLS]
 
     for side in (0, 1):
         @pl.when(to_col(side))
@@ -536,7 +535,6 @@
     for dx in (-1, 0, 1):
         for j in range(4):
             heat_copy(dx, j).wait_send()
-    result.wait()
     for c in range(CHUNKS):
         for j in range(4):
             one_copy(c, j).wait_send()
@@ -550,7 +548,11 @@
     factors = table_factors()
 
     def body(wave, lens, label, prior, attenuation, drain, diffusivity):
-        smem = pl.BlockSpec(memory_space=pltpu.SMEM)
+        vmem = pl.BlockSpec(memory_space=pltpu.VMEM)
+        anywhere = pl.BlockSpec(memory_space=pl.ANY)
+        def in_hbm(x):
+            return pltpu.with_memory_space_constraint(x, pltpu.HBM)
+
         hbm = pl.BlockSpec(memory_space=pltpu.HBM)
         dma = pltpu.SemaphoreType.DMA
         field, later = pl.pallas_call(
@@ -559,11 +561,11 @@
                 jax.ShapeDtypeStruct((ROWS, 2, COLS, OWN), F32),
                 jax.ShapeDtypeStruct((ROWS, COLS), F32),
             ),
-            in_specs=[hbm] * 4 + [smem] * 3 + [hbm] * 8,
-            out_specs=(hbm, hbm),
+            in_specs=[hbm] * 15,
+            out_specs=(anywhere, vmem),
             scratch_shapes=[
                 pltpu.VMEM((ROWS, COLS), jnp.int32), pltpu.VMEM((ROWS, COLS), jnp.int32), pltpu.VMEM((ROWS, COLS), F32),
-                pltpu.VMEM((ROWS, COLS), F32),
+                pltpu.SMEM((8,), F32), pltpu.SMEM((8,), F32), pltpu.SMEM((8,), F32),
                 pltpu.VMEM((2, ROWS, OWN, COLS), F32),
                 pltpu.VMEM((2, 12, COLS + 2 * PAD, OWN), F32),
                 pltpu.VMEM((2, 12, WIDEST + 2 * PAD, OWN), F32),
@@ -585,15 +587,15 @@
                 pltpu.VMEM((3, ROWS, 1, COLS), F32),
                 pltpu.VMEM((1, COLS), F32),
                 pltpu.VMEM((5, 16, 3 * COLS), F32),
-                dma((4,)), dma((2, ROWS)), dma((8,)), dma((2, CHUNKS)), dma((2, CHUNKS)), dma((2,)), dma((2,)), dma((2, 2)), dma((2, 2)),
+                dma((6,)), dma((2, ROWS)), dma((8,)), dma((2, CHUNKS)), dma((2, CHUNKS)), dma((2,)), dma((2,)), dma((2, 2)), dma((2, 2)),
                 dma((9,)), dma((9,)), dma((3,)), dma((3,)),
                 dma((CHUNKS, 4)), dma((CHUNKS, 4)), dma((PARTS, 4)), dma((PARTS, 4)), dma((3, 4)), dma((3, 4)),
             ],
             compiler_params=pltpu.CompilerParams(
-                collective_id=0, has_side_effects=True
+                collective_id=0, has_side_effects=True, vmem_limit_bytes=48 << 20
             ),
             name="march",
-        )(wave, lens, label, prior, attenuation, drain, diffusivity, *[jnp.asarray(f) for f in factors])
+        )(*[in_hbm(a) for a in (wave, lens, label, prior, attenuation, drain, diffusivity)], *[in_hbm(jnp.asarray(f)) for f in factors])
         return jnp.transpose(field, (1, 3, 0, 2)), later
 
     in_specs = (P(None, "harm", "tx", "ty"), P("tx", "ty"), P("tx", "ty"), P("tx", "ty"), P(), P(), P())

time: 74.2 us -> 72.3 us (0.974)
  Pallas kernels: 70.8 us -> 69.6 us
  local copies, waits for them, and re-layouts: 2.62 us -> 1.57 us
    pallas_call x1, Pallas kernels: 70.8 us -> 69.6 us  [body(): pl.pallas_call(kernel, out_shape=(jax.ShapeDtypeStruct((ROWS, 2, COLS, OW...]
    unnamed x4 -> x2, local copies, waits for them, and re-layouts: 2.62 us -> 1.57 us
where the time goes in v4:
time: 72.3 us; the launch traced here: 71.8 us
  Pallas kernels  69.6 us (96%)
  local copies, waits for them, and re-layouts  1.57 us (2%)
    pallas_call x1, Pallas kernels, body(): pl.pallas_call(kernel, out_shape=(jax.ShapeDtypeStruct((ROWS, 2, COLS, OW...  69.6 us
    unnamed x2, local copies, waits for them, and re-layouts  1.57 us

profile of v4, /device:TPU:6, one launch (start us, length us, event | category | flops | bytes accessed | tf_op | source)
XLA Modules:
  0.0 71.8 jit_solution(12546269957188554436)
XLA Ops:
  0.6 69.6 %march.1 = (f32[4,2,128,128]{3,2,1,0:T(8,128)S(1)}, f32[4,128]{1,0:T(4,128)S(1)}) custom-call(f32[2,128,4,128]{3,2,1,0:T(4,128)} %wave.1, s32[4,128]{1,0:T(4,128)} %lens_in.1, s32[4,128]{1,0:T(4,128)} %label_in.1, f32[4,128]{1,0:T(4,128)} %prior_in.1, f32[8]{0:T(128)} %attenuation_in.1, f32[8]{0:T(128)} %drain_in.1, f32[8]{0:T(128)} %diffusivity_in.1, ...), custom_call_target="tpu_custom_call" | custom-call | tf_op jit(solution)/shard_map/march/pallas_call | solution.py:558
  70.3 1.0 %copy.17 = f32[2,128,4,128]{3,2,1,0:T(4,128)} copy(f32[2,128,4,128]{1,3,0,2:T(8,128)S(1)} %bitcast.1) | data formatting | bytes 1048576
  71.3 0.6 copy.19

commit v5 on v4

--- a/solution.py
+++ b/solution.py
@@ -18,7 +18,7 @@
 ORDER = (1, 2, 0, 3, 4, 5, 6, 7, 8, 9)
 CHUNKS = len(SEGMENTS)
 WIDEST = 16
-EARLY_PARTS = 2
+EARLY_PARTS = 1
 PARTS = 4
 PART = COLS // PARTS
 PAD = 16
@@ -120,23 +120,24 @@
         S[:, :, 8:16] = jnp.zeros((2, 12, 8, OWN), F32)
         for dy in range(3):
             early[dy, 0] = jnp.zeros((4, ROWS, COLS), F32)
+        for row in range(ROWS):
+            heat_rows[0, row] = jnp.zeros((1, COLS), F32)
 
     @pl.when(ty == TY - 1)
     def _():
         S[:, :, PAD + COLS:PAD + COLS + 8] = jnp.zeros((2, 12, 8, OWN), F32)
         for dy in range(3):
             early[dy, 2] = jnp.zeros((4, ROWS, COLS), F32)
+        for row in range(ROWS):
+            heat_rows[2, row] = jnp.zeros((1, COLS), F32)
 
     barrier = pltpu.get_barrier_semaphore()
     for dy, dx in AROUND:
         @pl.when(inside(dy, dx))
         def _():
             pl.semaphore_signal(barrier, inc=1, device_id=(harm, tx + dy, ty + dx), device_id_type=pl.DeviceIdType.MESH)
-    for dx in (-1, 0, 1):
-        for j in range(4):
-            pl.semaphore_signal(
-                barrier, inc=1, device_id=(j, tx, (ty + dx + 4) % TY), device_id_type=pl.DeviceIdType.MESH
-            )
+    for j in range(4):
+        pl.semaphore_signal(barrier, inc=1, device_id=(j, tx, far_ty), device_id_type=pl.DeviceIdType.MESH)
 
     smalls = []
     for i, (a, b) in enumerate((
@@ -187,7 +188,7 @@
     def edges(at, count):
         return jnp.where(at == 0, 1, 0) + jnp.where(at == count - 1, 1, 0)
 
-    pl.semaphore_wait(barrier, (3 - edges(tx, TX)) * (3 - edges(ty, TY)) + 11)
+    pl.semaphore_wait(barrier, (3 - edges(tx, TX)) * (3 - edges(ty, TY)) + 3)
 
     def row_copy(side, c):
         return remote(
@@ -462,15 +463,26 @@
             (row, tx, far_ty),
         )
 
-    for dx in (-1, 0, 1):
-        for j in range(4):
-            heat_copy(dx, j).start()
+    def reached(dx):
+        return far_ty > 0 if dx < 0 else far_ty < TY - 1
+
+    for j in range(4):
+        heat_copy(0, j).start()
+    for dx in (-1, 1):
+        @pl.when(reached(dx))
+        def _():
+            for j in range(4):
+                heat_copy(dx, j).start()
     for c in range(EARLY_PARTS, PARTS):
         for j in range(4):
             two_copy(c, j).start()
-    for dx in (-1, 0, 1):
-        for row in range(ROWS):
-            heat_arrival(dx, row).wait_recv()
+    for row in range(ROWS):
+        heat_arrival(0, row).wait_recv()
+    for dx in (-1, 1):
+        @pl.when(inside(0, dx))
+        def _():
+            for row in range(ROWS):
+                heat_arrival(dx, row).wait_recv()
     for dx in range(3):
         for row in range(ROWS):
             late[1, dx, row:row + 1, :] = heat_rows[dx, row]
@@ -532,9 +544,13 @@
         @pl.when(inside(dy, 0))
         def _():
             late_copy(dy).wait_send()
-    for dx in (-1, 0, 1):
-        for j in range(4):
-            heat_copy(dx, j).wait_send()
+    for j in range(4):
+        heat_copy(0, j).wait_send()
+    for dx in (-1, 1):
+        @pl.when(reached(dx))
+        def _():
+            for j in range(4):
+                heat_copy(dx, j).wait_send()
     for c in range(CHUNKS):
         for j in range(4):
             one_copy(c, j).wait_send()

time: 72.3 us -> 71 us (0.982)
  the two profiles are of different devices: /device:TPU:6 before, /device:TPU:86 now
where the time goes in v5:
time: 71 us; the launch traced here: 70.9 us
  Pallas kernels  68.7 us (97%)
  local copies, waits for them, and re-layouts  1.57 us (2%)
    pallas_call x1, Pallas kernels, body(): pl.pallas_call(kernel, out_shape=(jax.ShapeDtypeStruct((ROWS, 2, COLS, OW...  68.7 us
    unnamed x2, local copies, waits for them, and re-layouts  1.57 us

profile of v5, /device:TPU:86, one launch (start us, length us, event | category | flops | bytes accessed | tf_op | source)
XLA Modules:
  0.0 70.9 jit_solution(11292074119867620823)
XLA Ops:
  0.6 68.7 %march.1 = (f32[4,2,128,128]{3,2,1,0:T(8,128)S(1)}, f32[4,128]{1,0:T(4,128)S(1)}) custom-call(f32[2,128,4,128]{3,2,1,0:T(4,128)} %wave.1, s32[4,128]{1,0:T(4,128)} %lens_in.1, s32[4,128]{1,0:T(4,128)} %label_in.1, f32[4,128]{1,0:T(4,128)} %prior_in.1, f32[8]{0:T(128)} %attenuation_in.1, f32[8]{0:T(128)} %drain_in.1, f32[8]{0:T(128)} %diffusivity_in.1, ...), custom_call_target="tpu_custom_call" | custom-call | tf_op jit(solution)/shard_map/march/pallas_call | solution.py:574
  69.3 1.0 %copy.17 = f32[2,128,4,128]{3,2,1,0:T(4,128)} copy(f32[2,128,4,128]{1,3,0,2:T(8,128)S(1)} %bitcast.1) | data formatting | bytes 1048576
  70.3 0.6 copy.19
